TPU v7x, 32 devices: a whole 2x2x4 slice. The times are simulated.
32 devices in a mesh: sector: 8 (over z, core), cap: 4 (over y, x).
Axes of the slice: x: 2, y: 2, z: 4, core: 2. Of those that a mesh axis runs over, the one named last changes fastest.
Arguments:
- start_value: float32 [64, 32, 2048], P('sector', None, 'cap'), may hold values from 0 to 4
- firm_mass: float32 [64, 32, 2048], P('sector', None, 'cap'), may hold values from 0.1 to 10
- survive: int32 [64, 32, 2048], P('sector', None, 'cap'), may hold values from 0 to 1, as said below
- exit_index: int32 [64], P('sector'), may hold values from 0 to 8
- demand: float32 [64], P('sector'), may hold values from 0.3 to 90, as said below
- transition: float32 [32, 32], replicated, may hold values from 0 to 1, as said below
- install_cost: float32 [2048], P('cap'), may hold values from 0 to 1
Outputs:
- final_value: float32 [64, 32, 2048], P('sector', None, 'cap')
- rel_prices: float32 [64], P('sector')
Inputs may be any that keep to these rules, and one draw needn't show every extreme that they name: `survive`: 0 or 1; the share of ones differs from sector to sector, from about a tenth to all. `demand`: positive, rising over the sectors by some thirty times. `transition`: entries positive, every row sums to one.
All inputs are finite; a program needn't handle non-finite values.
Results may differ from a plain program's by a relative error of at most 0.0003.
Values sent between devices are 32-bit elements; how exact they have to be, the bound alone decides.
A program may use at most 64 MiB of HBM per device.

v0:
```python
import functools
import math

import jax
import jax.numpy as jnp
from jax import lax
from jax.experimental import pallas as pl
from jax.experimental.pallas import tpu as pltpu
from jax.sharding import PartitionSpec as P

SWEEPS = 2
CHUNK_SLOTS = 8
SLOTS = 16
MERGED = 16
RANGES = 4
MERGED_RANGES = 2
NEG = -1e30
LOG_TEN = math.log(10.0)


def capital_of(positions, total):
    return 0.2 * jnp.exp(LOG_TEN * positions.astype(jnp.float32) / (total - 1))


def charge_of(cap_now, cap_next, row_ids, col_ids):
    invest = cap_next - 0.9 * cap_now
    fixed = jnp.where(row_ids == col_ids, 0.0, 1.5 * cap_now)
    return invest + invest * invest / cap_now + fixed


def best_reply(forward_rows, row_first, row_count):
    total_rows, total_cols = forward_rows.shape
    cap_of = functools.partial(capital_of, total=total_cols)
    col_block = math.gcd(total_cols, 2048)
    row_block = math.gcd(row_count, 512)
    grp_limit = max(1, (1 << 24) // (row_block * col_block))
    grp_size = math.gcd(total_rows, 1 << min(total_rows, grp_limit).bit_length() - 1)
    groups = forward_rows.reshape(total_rows // grp_size, grp_size, total_cols)

    def one_group(group):
        row_ids = row_first + jnp.arange(row_count, dtype=jnp.int32)
        cap_rows = cap_of(row_ids)
        col_ids = jnp.arange(total_cols, dtype=jnp.int32)
        cap_cols = cap_of(col_ids)
        charge = charge_of(cap_rows[:, None], cap_cols[None, :], row_ids[:, None], col_ids[None, :])
        return jnp.max(group[:, None, :] - charge[None], axis=2)

    return lax.map(one_group, groups).reshape(total_rows, row_count)


def gather_blocks(block, axis_name):
    count = lax.axis_size(axis_name)
    me = lax.axis_index(axis_name)
    parts = [block]
    for off in range(1, count):
        parts.append(lax.ppermute(block, axis_name, [(d, (d + off) % count) for d in range(count)]))
    return jnp.take(jnp.stack(parts), (me - jnp.arange(count) + count) % count, axis=0)


def dense_sweeps(start_value, firm_mass, survive, exit_index, demand, transition, install_cost):
    sec_dev, prod_count, cap_dev = start_value.shape
    sectors_all = sec_dev * lax.axis_size("sector")
    row_first = lax.axis_index("cap") * cap_dev
    prod_index = jnp.arange(prod_count, dtype=jnp.int32)
    total = cap_dev * lax.axis_size("cap")
    capital = capital_of(row_first + jnp.arange(cap_dev, dtype=jnp.int32), total)
    log_prod = -0.5 + prod_index.astype(jnp.float32) / (prod_count - 1)
    output = jnp.exp(log_prod)[:, None] * capital[None, :] ** 0.6
    scrap = 0.3 * capital
    live = (survive == 1) & (prod_index[None, :, None] >= exit_index[:, None, None])
    values = start_value
    relative = jnp.zeros((sec_dev,), jnp.float32)
    for sweep in range(SWEEPS):
        staying = jnp.where(live, jax.nn.sigmoid((values - scrap) / 0.5), 0.0)
        partial_value = jnp.sum(firm_mass * staying * output, axis=(1, 2))
        supply = 1.0 + jnp.sum(gather_blocks(partial_value, "cap"), axis=0) / (prod_count * total)
        prices = jnp.sqrt(demand / supply)
        root_sum = jnp.sum(gather_blocks(jnp.sqrt(prices), "sector"))
        price_index = (root_sum / sectors_all) ** 2
        relative = prices / price_index
        continuation = jnp.where(live, jnp.maximum(values, scrap), scrap)
        expect = jnp.einsum(
            "zw,swk->szk", transition, continuation, precision=lax.Precision.HIGHEST
        )
        forward_value = 0.9 * expect - install_cost[None, None, :]
        blocks = gather_blocks(forward_value, "cap")
        rows = jnp.moveaxis(blocks, 0, 2).reshape(sec_dev * prod_count, total)
        best = best_reply(rows, row_first, cap_dev).reshape(sec_dev, prod_count, cap_dev)
        values = jnp.where(live, relative[:, None, None] * output + best, scrap)
    return (values, relative)


def rows_of(step):
    return pl.ds(pl.multiple_of(step * 8, 8), 8)


def all_max(parts):
    return functools.reduce(jnp.maximum, parts)


def bases(tot_ref, count, sub, first, last):
    before, after = [], []
    for e in range(count):
        rows = [tot_ref[e, a:a + 1, :] for a in range(8)]
        if e < count - 1:
            before.append(all_max([jnp.where(sub > a, rows[a], NEG) for a in range(7)]))
        if e > 0:
            after.append(all_max([jnp.where(sub < a, rows[a], NEG) for a in range(1, 8)]))
    return before, after


def counts_before(tot_ref, counts, sub):
    tot_ref[0] = counts
    base = jnp.zeros_like(counts)
    for a in range(7):
        base = base + jnp.where(sub > a, tot_ref[0, a:a + 1, :], 0.0)
    return base


def useful(points, runs, sufs, afters):
    keep = None
    for e in range(len(runs)):
        good = (points[e] > runs[e]) & (points[e + 1] > jnp.maximum(sufs[e], afters[e]))
        keep = good if keep is None else keep | good
    return keep


def sweeps_kernel(n_sec, n_cap, start_hbm, mass_hbm, survive_hbm, exit_hbm, demand_hbm, trans_hbm, cost_hbm,
                  out_ref, cand_ref, rel_ref, flag_ref,
                  start_v, mass_v, survive_v, exit_v, demand_v, trans_v, cost_v,
                  nat_ref, val_ref, live_ref, g_ref, suf_ref, best_ref, col_ref, qt_ref,
                  weight_ref, ones_ref, tot_ref, l1_ref, pick_ref, zsum_ref, price_ref,
                  msg_ref, gat_ref, dem_ref, dems_ref, flg_ref, flgs_ref, pay_ref, pays_ref, size_ref,
                  in_sem, msg_send, msg_recv, dem_send, dem_recv, flg_send, flg_recv, pay_send, pay_recv):
    sec_dev, prods, cap_dev = start_v.shape
    total = cap_dev * n_cap
    steps = cap_dev // 8
    tiles = sec_dev * prods // 128
    tile_sec = 128 // prods
    lanes = tiles * 128
    col_tiles = cap_dev // 128
    n_dev = n_sec * n_cap
    me_cap = lax.axis_index("cap")
    me_sec = lax.axis_index("sector")
    me = me_sec * n_cap + me_cap
    my_row = me_cap * n_sec + me_sec
    mesh_id = pl.DeviceIdType.MESH
    f32 = jnp.float32

    def device(index):
        return {"sector": index // n_cap, "cap": lax.rem(index, n_cap)}

    barrier = pltpu.get_barrier_semaphore()

    def greet(off, carry):
        pl.semaphore_signal(barrier, inc=1, device_id=device(lax.rem(me + off, n_dev)), device_id_type=mesh_id)
        return carry

    lax.fori_loop(1, n_dev, greet, 0)
    loads = []
    for at, (src, dst) in enumerate((
        (trans_hbm, trans_v), (cost_hbm, cost_v), (exit_hbm, exit_v), (demand_hbm, demand_v),
        (mass_hbm, mass_v), (survive_hbm, survive_v), (start_hbm, start_v),
    )):
        loads.append(pltpu.make_async_copy(src, dst, in_sem.at[at]))
        loads[-1].start()

    sub = lax.broadcasted_iota(jnp.int32, (8, 128), 0)
    subf = sub.astype(f32)
    lane = lax.broadcasted_iota(jnp.int32, (1, 128), 1)
    lane_prod = lax.rem(lane, prods)
    lane_sec = lane // prods
    ends = [0.5 * 10.0 ** (e / RANGES) for e in range(RANGES + 1)]
    ends[0] *= 1.0 - 1e-5
    ends[-1] *= 1.0 + 1e-5
    first = me_cap * cap_dev
    CAP, SLOPE, POW, GADD, SQUARE = range(5)

    row = lax.broadcasted_iota(jnp.int32, (cap_dev, 128), 0)
    place = first + lax.rem(row, 8) * steps + row // 8
    capital = capital_of(place, total)
    col_ref[CAP] = capital
    col_ref[SLOPE] = 1.0 / capital
    col_ref[POW] = jnp.exp(0.6 * (math.log(0.2) + LOG_TEN * place.astype(f32) / (total - 1)))
    col_ref[SQUARE] = capital * capital
    for e in range(RANGES + 1):
        qt_ref[e] = capital * capital * ends[e]
    edge = [first + cap_dev - 1, first]
    t_low, t_high = [1.0 / capital_of(jnp.full((8, 128), at, jnp.int32), total) for at in edge]
    t_low, t_high = t_low * (1.0 - 1e-5), t_high * (1.0 + 1e-5)
    log_low, log_high = jnp.log(t_low), jnp.log(t_high)
    near = [t_low] + [
        jnp.exp(log_low + (log_high - log_low) * (e / MERGED_RANGES)) for e in range(1, MERGED_RANGES)
    ] + [t_high]
    prod_row = jnp.exp(-0.5 + lane_prod.astype(f32) / (prods - 1))
    big_r = lax.broadcasted_iota(jnp.int32, (128, 128), 0)
    big_c = lax.broadcasted_iota(jnp.int32, (128, 128), 1)
    same = big_r // prods == big_c // prods
    ones_ref[...] = jnp.where(same, 1.0, 0.0)

    loads[0].wait()
    spot_r = lax.broadcasted_iota(jnp.int32, (128, prods), 0)
    spot_c = lax.broadcasted_iota(jnp.int32, (128, prods), 1)
    spot = jnp.where(lax.rem(spot_r, prods) == spot_c, 1.0, 0.0)
    dims = (((1,), (1,)), ((), ()))
    half = lax.dot_general(spot, trans_v[...], dims, precision=lax.Precision.HIGHEST, preferred_element_type=f32)
    full = lax.dot_general(half, spot, dims, precision=lax.Precision.HIGHEST, preferred_element_type=f32)
    weight = jnp.where(same, 0.9 * full, 0.0)
    top = weight.astype(jnp.bfloat16)
    low = (weight - top.astype(f32)).astype(jnp.bfloat16)
    weight_ref[0:128, 0:128] = top
    weight_ref[128:256, 0:128] = top
    weight_ref[0:128, 128:256] = low
    weight_ref[128:256, 128:256] = jnp.zeros_like(low)

    loads[1].wait()
    for at in range(0, cap_dev, 128):
        nat_ref[0, at:at + 128, :] = jnp.broadcast_to(cost_v[:, at:at + 128], (128, 128)).T

    def add_step(i, carry):
        rows = rows_of(i)
        col_ref[GADD, rows, :] = 0.8 * col_ref[CAP, rows, :] - nat_ref[0, pl.ds(i, 8, stride=steps), :]
        return carry

    lax.fori_loop(0, steps, add_step, 0, unroll=4)

    loads[2].wait()
    loads[3].wait()
    exit_rows, demand_rows = [], []
    for t in range(tiles):
        exit_row = jnp.zeros((1, 128), jnp.int32)
        demand_row = jnp.zeros((1, 128), f32)
        for s in range(tile_sec):
            exit_row = jnp.where(lane_sec == s, exit_v[t * tile_sec + s], exit_row)
            demand_row = jnp.where(lane_sec == s, demand_v[t * tile_sec + s], demand_row)
        exit_rows.append(lane_prod >= exit_row)
        demand_rows.append(demand_row)
    dem_ref[...] = jnp.concatenate(demand_rows, axis=1)

    loads[4].wait()
    loads[5].wait()
    for t in range(tiles):
        secs = slice(t * tile_sec, (t + 1) * tile_sec)
        for at in range(0, cap_dev, 128):
            block = jnp.where(survive_v[secs, :, at:at + 128] == 1, mass_v[secs, :, at:at + 128], 0.0)
            nat_ref[t, at:at + 128, :] = block.reshape(128, 128).T

    for t in range(tiles):
        def live_step(i, carry, t=t):
            live_ref[t, rows_of(i), :] = jnp.where(exit_rows[t], nat_ref[t, pl.ds(i, 8, stride=steps), :], 0.0)
            return carry

        lax.fori_loop(0, steps, live_step, 0, unroll=4)
    loads[6].wait()
    for t in range(tiles):
        secs = slice(t * tile_sec, (t + 1) * tile_sec)
        for at in range(0, cap_dev, 128):
            nat_ref[t, at:at + 128, :] = start_v[secs, :, at:at + 128].reshape(128, 128).T

    def weigh(t, rows, value):
        scrap = 0.3 * col_ref[CAP, rows, :]
        stay = 1.0 / (1.0 + jnp.exp(2.0 * (scrap - value)))
        return live_ref[t, rows, :] * stay * col_ref[POW, rows, :]

    def send_supply(sweep, sums):
        grouped = jnp.dot(
            jnp.concatenate([part * prod_row for part in sums], axis=0), ones_ref[...],
            precision=lax.Precision.HIGHEST, preferred_element_type=f32)
        zsum_ref[...] = grouped
        for t in range(tiles):
            line = zsum_ref[t * 8:t * 8 + 1, :]
            for a in range(1, 8):
                line = line + zsum_ref[t * 8 + a:t * 8 + a + 1, :]
            msg_ref[sweep, :, t * 128:(t + 1) * 128] = line

        def post(off, carry):
            message(sweep, off).start()
            return carry

        lax.fori_loop(1, n_dev, post, 0)
        gat_ref[sweep, pl.ds(my_row, 1), :] = msg_ref[sweep]

    def message(sweep, off):
        return pltpu.make_async_remote_copy(
            src_ref=msg_ref.at[sweep], dst_ref=gat_ref.at[sweep, pl.ds(my_row, 1), :],
            send_sem=msg_send.at[sweep], recv_sem=msg_recv.at[sweep],
            device_id=device(lax.rem(me + off, n_dev)), device_id_type=mesh_id)

    def wait_rows(count, width, sem):
        view = size_ref.at[pl.ds(0, count), :, pl.ds(0, width)]
        pltpu.make_async_copy(view, view, sem).wait()

    def prices_row(sweep):
        wait_rows(n_dev - 1, lanes + 128, msg_recv.at[sweep])
        every = gat_ref[sweep, 0:n_sec, 0:lanes]
        for c in range(1, n_cap):
            every = every + gat_ref[sweep, c * n_sec:(c + 1) * n_sec, 0:lanes]
        supply = 1.0 + every / (prods * total)
        prices = jnp.sqrt(dems_ref[...] / supply)
        price_ref[...] = prices
        mean = jnp.sum(jnp.sqrt(prices), keepdims=True) / (lanes * n_sec)
        return price_ref[pl.ds(me_sec, 1), :] / (mean * mean)

    def forward(t):
        def chunk(at, carry):
            rows = pl.ds(pl.multiple_of(at * 128, 128), 128)
            cont = jnp.maximum(val_ref[t, rows, :], 0.3 * col_ref[CAP, rows, :])
            upper = cont.astype(jnp.bfloat16)
            lower = (cont - upper.astype(f32)).astype(jnp.bfloat16)
            both = jnp.dot(jnp.concatenate([upper, lower], axis=1), weight_ref[...], preferred_element_type=f32)
            g_ref[t, rows, :] = both[:, 0:128] + both[:, 128:256] + col_ref[GADD, rows, :]
            return carry

        lax.fori_loop(0, col_tiles, chunk, 0)

    def collect(rows_list, rank_rows, count):
        picks = [jnp.full((8, 128), NEG, f32) for _ in range(count // 8)]
        squares = [jnp.zeros((8, 128), f32) for _ in range(count // 8)]
        for (gain, square), rank in zip(rows_list, rank_rows):
            for h in range(count // 8):
                here = rank == subf + 8.0 * h
                picks[h] = jnp.where(here, gain, picks[h])
                squares[h] = jnp.where(here, square, squares[h])
        return picks, squares

    def prune(sweep, t):
        def back(at, runs):
            i = steps - 1 - at
            rows = rows_of(i)
            gain = g_ref[t, rows, :]
            points = [gain - qt_ref[e, rows, :] for e in range(RANGES + 1)]
            for e in range(RANGES):
                suf_ref[e, rows, :] = runs[e + 1]
            return tuple(jnp.maximum(run, point) for run, point in zip(runs, points))

        runs = lax.fori_loop(0, steps, back, (jnp.full((8, 128), NEG, f32),) * (RANGES + 1), unroll=4)
        for e in range(RANGES + 1):
            tot_ref[e] = runs[e]
        before, after = bases(tot_ref, RANGES + 1, sub, 0, 7)

        def ahead(i, carry):
            runs, counts, gains, squares = carry
            rows = rows_of(i)
            gain = g_ref[t, rows, :]
            square = col_ref[SQUARE, rows, :]
            points = [gain - qt_ref[e, rows, :] for e in range(RANGES + 1)]
            keep = useful(points, runs, [suf_ref[e, rows, :] for e in range(RANGES)], after)
            runs = tuple(jnp.maximum(run, point) for run, point in zip(runs, points))
            gains = tuple(jnp.where(keep, new, old) for new, old in zip((gain,) + gains, gains))
            squares = tuple(jnp.where(keep, new, old) for new, old in zip((square,) + squares, squares))
            return runs, counts + jnp.where(keep, 1.0, 0.0), gains, squares

        zero = jnp.zeros((8, 128), f32)
        runs, counts, gains, squares = lax.fori_loop(
            0, steps, ahead, (tuple(before), zero, (zero,) * CHUNK_SLOTS, (zero,) * CHUNK_SLOTS), unroll=4)
        base = counts_before(tot_ref, counts, sub)
        for p in range(CHUNK_SLOTS):
            l1_ref[0, p * 8:(p + 1) * 8, :] = gains[p]
            l1_ref[1, p * 8:(p + 1) * 8, :] = squares[p]
            l1_ref[2, p * 8:(p + 1) * 8, :] = jnp.where(counts > p, base + counts - (p + 1.0), -1.0)
        spots = range(CHUNK_SLOTS * 8)
        picks, squares = collect(
            [(l1_ref[0, r:r + 1, :], l1_ref[1, r:r + 1, :]) for r in spots],
            [l1_ref[2, r:r + 1, :] for r in spots], SLOTS)
        mine = pl.ds(pl.multiple_of(me_cap * SLOTS, SLOTS), SLOTS)
        for h in range(SLOTS // 8):
            pay_ref[sweep, t, 0, h * 8:(h + 1) * 8, :] = picks[h]
            pay_ref[sweep, t, 1, h * 8:(h + 1) * 8, :] = squares[h]
        for off in range(1, n_cap):
            payment(sweep, t, off).start()
        pays_ref[sweep, t, :, mine, :] = pay_ref[sweep, t]
        return jnp.where((counts > CHUNK_SLOTS) | (base + counts > SLOTS), 1.0, 0.0)

    def payment(sweep, t, off):
        mine = pl.ds(pl.multiple_of(me_cap * SLOTS, SLOTS), SLOTS)
        return pltpu.make_async_remote_copy(
            src_ref=pay_ref.at[sweep, t], dst_ref=pays_ref.at[sweep, t, :, mine, :],
            send_sem=pay_send.at[sweep, t], recv_sem=pay_recv.at[sweep, t],
            device_id={"cap": lax.rem(me_cap + off, n_cap)}, device_id_type=mesh_id)

    def pay_view(sweep, t):
        return pays_ref.at[sweep, t, :, pl.ds(0, (n_cap - 1) * SLOTS), :]

    def merge(sweep, t):
        pltpu.make_async_copy(pay_view(sweep, t), pay_view(sweep, t), pay_recv.at[sweep, t]).wait()
        hops = n_cap * SLOTS // 8

        def line(i):
            spots = pl.ds(i, 8, stride=hops)
            return pays_ref[sweep, t, 0, spots, :], pays_ref[sweep, t, 1, spots, :]

        def back(at, runs):
            i = hops - 1 - at
            gain, square = line(i)
            points = [gain - square * near[e] for e in range(MERGED_RANGES + 1)]
            for e in range(MERGED_RANGES):
                suf_ref[e, rows_of(i), :] = runs[e + 1]
            return tuple(jnp.maximum(run, point) for run, point in zip(runs, points))

        runs = lax.fori_loop(0, hops, back, (jnp.full((8, 128), NEG, f32),) * (MERGED_RANGES + 1), unroll=8)
        for e in range(MERGED_RANGES + 1):
            tot_ref[e] = runs[e]
        before, after = bases(tot_ref, MERGED_RANGES + 1, sub, 0, 7)

        def ahead(i, carry):
            runs, counts = carry
            gain, square = line(i)
            points = [gain - square * near[e] for e in range(MERGED_RANGES + 1)]
            keep = useful(points, runs, [suf_ref[e, rows_of(i), :] for e in range(MERGED_RANGES)], after)
            runs = tuple(jnp.maximum(run, point) for run, point in zip(runs, points))
            pick_ref[0, rows_of(i), :] = jnp.where(keep, counts, NEG)
            return runs, counts + jnp.where(keep, 1.0, 0.0)

        runs, counts = lax.fori_loop(0, hops, ahead, (tuple(before), jnp.zeros((8, 128), f32)), unroll=8)
        base = counts_before(tot_ref, counts, sub)
        for i in range(hops):
            pick_ref[0, i * 8:(i + 1) * 8, :] = pick_ref[0, i * 8:(i + 1) * 8, :] + base
        spots = [(i, a) for i in range(hops) for a in range(8)]
        picks, squares = collect(
            [(pays_ref[sweep, t, 0, a * hops + i:a * hops + i + 1, :],
              pays_ref[sweep, t, 1, a * hops + i:a * hops + i + 1, :]) for i, a in spots],
            [pick_ref[0, i * 8 + a:i * 8 + a + 1, :] for i, a in spots], MERGED)
        for h in range(MERGED // 8):
            pick_ref[1, h * 8:(h + 1) * 8, :] = picks[h]
            pick_ref[2, h * 8:(h + 1) * 8, :] = squares[h]
        return jnp.where(base + counts > MERGED, 1.0, 0.0)

    def reply(t):
        gains = [jnp.broadcast_to(pick_ref[1, c:c + 1, :], (8, 128)) for c in range(MERGED)]
        squares = [jnp.broadcast_to(pick_ref[2, c:c + 1, :], (8, 128)) for c in range(MERGED)]

        def one(i, carry):
            rows = rows_of(i)
            slope = col_ref[SLOPE, rows, :]
            capital = col_ref[CAP, rows, :]
            moved = all_max([gain - square * slope for gain, square in zip(gains, squares)])
            best_ref[t, rows, :] = jnp.maximum(moved - 1.41 * capital, g_ref[t, rows, :] - 0.91 * capital)
            return carry

        lax.fori_loop(0, steps, one, 0, unroll=4)

    sums = []
    for t in range(tiles):
        def open_step(i, acc, t=t):
            rows = rows_of(i)
            value = jnp.where(live_ref[t, rows, :] > 0.0, nat_ref[t, pl.ds(i, 8, stride=steps), :],
                              0.3 * col_ref[CAP, rows, :])
            val_ref[t, rows, :] = value
            return acc + weigh(t, rows, value)

        sums.append(lax.fori_loop(0, steps, open_step, jnp.zeros((8, 128), f32), unroll=8))
    pl.semaphore_wait(barrier, n_dev - 1)
    dem_copies = []
    for off in range(1, n_sec):
        dem_copies.append(pltpu.make_async_remote_copy(
            src_ref=dem_ref, dst_ref=dems_ref.at[pl.ds(me_sec, 1), :], send_sem=dem_send, recv_sem=dem_recv,
            device_id={"sector": lax.rem(me_sec + off, n_sec)}, device_id_type=mesh_id))
        dem_copies[-1].start()
    dems_ref[pl.ds(me_sec, 1), :] = dem_ref[...]
    msg_ref[0, :, lanes:lanes + 128] = jnp.zeros((1, 128), f32)

    def flag_row(flags):
        tot_ref[0] = flags
        return all_max([tot_ref[0, a:a + 1, :] for a in range(8)])

    late = None
    for sweep in range(SWEEPS):
        send_supply(sweep, sums)
        flags = jnp.zeros((8, 128), f32)
        for t in range(tiles):
            forward(t)
            flags = jnp.maximum(flags, prune(sweep, t))
        if sweep == SWEEPS - 1:
            flg_ref[...] = flag_row(flags)

            def report(off, carry):
                pltpu.make_async_remote_copy(
                    src_ref=flg_ref, dst_ref=flgs_ref.at[pl.ds(my_row, 1), :], send_sem=flg_send, recv_sem=flg_recv,
                    device_id=device(lax.rem(me + off, n_dev)), device_id_type=mesh_id).start()
                return carry

            lax.fori_loop(1, n_dev, report, 0)
            flgs_ref[pl.ds(my_row, 1), :] = flg_ref[...]
        late = jnp.zeros((8, 128), f32)
        for t in range(tiles):
            late = jnp.maximum(late, merge(sweep, t))
            reply(t)
        if sweep == 0:
            msg_ref[1, :, lanes:lanes + 128] = flag_row(jnp.maximum(flags, late))
            wait_rows(n_sec - 1, lanes, dem_recv)
        relative = prices_row(sweep)
        if sweep == 0:
            sums = []
            for t in range(tiles):
                scale = relative[:, t * 128:(t + 1) * 128] * prod_row

                def next_step(i, acc, t=t, scale=scale):
                    rows = rows_of(i)
                    value = jnp.where(live_ref[t, rows, :] > 0.0,
                                      scale * col_ref[POW, rows, :] + best_ref[t, rows, :],
                                      0.3 * col_ref[CAP, rows, :])
                    val_ref[t, rows, :] = value
                    return acc + weigh(t, rows, value)

                sums.append(lax.fori_loop(0, steps, next_step, jnp.zeros((8, 128), f32), unroll=8))
    for s in range(sec_dev):
        rel_ref[s] = relative[0, s * prods]
    for t in range(tiles):
        scale = relative[:, t * 128:(t + 1) * 128] * prod_row

        def last_step(i, carry, t=t, scale=scale):
            rows = rows_of(i)
            nat_ref[t, pl.ds(i, 8, stride=steps), :] = jnp.where(
                live_ref[t, rows, :] > 0.0, scale * col_ref[POW, rows, :] + best_ref[t, rows, :],
                0.3 * col_ref[CAP, rows, :])
            return carry

        lax.fori_loop(0, steps, last_step, 0, unroll=8)
        secs = slice(t * tile_sec, (t + 1) * tile_sec)
        for at in range(0, cap_dev, 128):
            out_ref[secs, :, at:at + 128] = nat_ref[t, at:at + 128, :].T.reshape(tile_sec, prods, 128)
    cand_ref[...] = pays_ref[SWEEPS - 1]
    wait_rows(n_dev - 1, 128, flg_recv)
    bad = jnp.max(jnp.maximum(jnp.max(flgs_ref[...], axis=0, keepdims=True),
                              jnp.max(gat_ref[1, :, lanes:lanes + 128], axis=0, keepdims=True)))
    flag_ref[0] = jnp.where(bad > 0.0, 2, jnp.where(jnp.max(late) > 0.0, 1, 0)).astype(jnp.int32)

    for sweep in range(SWEEPS):
        wait_rows(n_dev - 1, lanes + 128, msg_send.at[sweep])
        for t in range(tiles):
            pltpu.make_async_copy(pay_view(sweep, t), pay_view(sweep, t), pay_send.at[sweep, t]).wait()
    wait_rows(n_dev - 1, 128, flg_send)
    wait_rows(n_sec - 1, lanes, dem_send)


def pruned_sweeps(start_value, firm_mass, survive, exit_index, demand, transition, install_cost):
    n_sec, n_cap = lax.axis_size("sector"), lax.axis_size("cap")
    sec_dev, prods, cap_dev = start_value.shape
    lanes = sec_dev * prods
    tiles = lanes // 128
    n_dev = n_sec * n_cap
    far = pl.BlockSpec(memory_space=pl.ANY)
    vmem = pl.BlockSpec(memory_space=pltpu.VMEM)
    smem = pl.BlockSpec(memory_space=pltpu.SMEM)
    f32 = jnp.float32
    dma = pltpu.SemaphoreType.DMA
    pack = max(RANGES, MERGED_RANGES)
    return pl.pallas_call(
        functools.partial(sweeps_kernel, n_sec, n_cap),
        out_shape=(
            jax.ShapeDtypeStruct(start_value.shape, f32),
            jax.ShapeDtypeStruct((tiles, 2, n_cap * SLOTS, 128), f32),
            jax.ShapeDtypeStruct((sec_dev,), f32),
            jax.ShapeDtypeStruct((1,), jnp.int32),
        ),
        in_specs=[far] * 7,
        out_specs=(vmem, vmem, smem, smem),
        scratch_shapes=[
            pltpu.VMEM(start_value.shape, f32),
            pltpu.VMEM(start_value.shape, f32),
            pltpu.VMEM(start_value.shape, jnp.int32),
            pltpu.SMEM((sec_dev,), jnp.int32),
            pltpu.SMEM((sec_dev,), f32),
            pltpu.VMEM((prods, prods), f32),
            pltpu.VMEM((1, cap_dev), f32),
            pltpu.VMEM((tiles, cap_dev, 128), f32),
            pltpu.VMEM((tiles, cap_dev, 128), f32),
            pltpu.VMEM((tiles, cap_dev, 128), f32),
            pltpu.VMEM((tiles, cap_dev, 128), f32),
            pltpu.VMEM((pack, max(cap_dev, n_cap * SLOTS), 128), f32),
            pltpu.VMEM((tiles, cap_dev, 128), f32),
            pltpu.VMEM((5, cap_dev, 128), f32),
            pltpu.VMEM((RANGES + 1, cap_dev, 128), f32),
            pltpu.VMEM((256, 256), jnp.bfloat16),
            pltpu.VMEM((128, 128), f32),
            pltpu.VMEM((pack + 1, 8, 128), f32),
            pltpu.VMEM((3, CHUNK_SLOTS * 8, 128), f32),
            pltpu.VMEM((3, max(MERGED, n_cap * SLOTS), 128), f32),
            pltpu.VMEM((tiles * 8, 128), f32),
            pltpu.VMEM((n_sec, lanes), f32),
            pltpu.VMEM((SWEEPS, 1, lanes + 128), f32),
            pltpu.VMEM((SWEEPS, n_dev, lanes + 128), f32),
            pltpu.VMEM((1, lanes), f32),
            pltpu.VMEM((n_sec, lanes), f32),
            pltpu.VMEM((1, 128), f32),
            pltpu.VMEM((n_dev, 128), f32),
            pltpu.VMEM((SWEEPS, tiles, 2, SLOTS, 128), f32),
            pltpu.VMEM((SWEEPS, tiles, 2, n_cap * SLOTS, 128), f32),
            pltpu.VMEM((n_dev - 1, 1, lanes + 128), f32),
            dma((7,)),
            dma((SWEEPS,)), dma((SWEEPS,)), dma, dma, dma, dma,
            dma((SWEEPS, tiles)), dma((SWEEPS, tiles)),
        ],
        compiler_params=pltpu.CompilerParams(
            collective_id=0, has_side_effects=True, vmem_limit_bytes=48 * 1024 * 1024
        ),
    )(start_value, firm_mass, survive, exit_index, demand, transition, install_cost[None, :])


def all_candidates(values, candidates, relative, survive, exit_index):
    sec_dev, prods, cap_dev = values.shape
    total = cap_dev * lax.axis_size("cap")
    capital = capital_of(lax.axis_index("cap") * cap_dev + jnp.arange(cap_dev, dtype=jnp.int32), total)
    prod_index = jnp.arange(prods, dtype=jnp.int32)
    output = jnp.exp(-0.5 + prod_index.astype(jnp.float32) / (prods - 1))[:, None] * capital[None, :] ** 0.6
    live = (survive == 1) & (prod_index[None, :, None] >= exit_index[:, None, None])
    flat = jnp.moveaxis(candidates, 0, 2).reshape(2, candidates.shape[2], sec_dev, prods)

    def one(best, pair):
        return jnp.maximum(best, pair[0][:, :, None] - pair[1][:, :, None] / capital), None

    moved, _ = lax.scan(one, jnp.full(values.shape, NEG, jnp.float32), (flat[0], flat[1]))
    again = relative[:, None, None] * output + (moved - 1.41 * capital)
    return jnp.where(live, jnp.maximum(values, again), values)


def on_device(start_value, firm_mass, survive, exit_index, demand, transition, install_cost):
    args = (start_value, firm_mass, survive, exit_index, demand, transition, install_cost)
    sec_dev, prods, cap_dev = start_value.shape
    if 128 % prods or prods % 8 or sec_dev * prods % 128 or cap_dev % 128 or min(
            lax.axis_size("sector"), lax.axis_size("cap")) < 2:
        return dense_sweeps(*args)
    values, candidates, relative, state = pruned_sweeps(*args)
    return lax.switch(
        state[0],
        (
            lambda: (values, relative),
            lambda: (all_candidates(values, candidates, relative, survive, exit_index), relative),
            lambda: dense_sweeps(*args),
        ),
    )


def solution(mesh):
    return jax.shard_map(
        on_device,
        mesh=mesh,
        in_specs=(
            P("sector", None, "cap"),
            P("sector", None, "cap"),
            P("sector", None, "cap"),
            P("sector"),
            P("sector"),
            P(),
            P("cap"),
        ),
        out_specs=(P("sector", None, "cap"), P("sector")),
        check_vma=False,
    )
```

profile of v0, /device:TPU:0, one launch (start us, length us, event | category | flops | bytes accessed | tf_op | source)
XLA Modules:
  0.0 28.9 jit_solution(17497240310729938970)
XLA Ops:
  0.6 25.4 %shard_map.92 = (f32[8,32,512]{2,1,0:T(8,128)S(1)}, f32[2,2,64,128]{3,2,1,0:T(8,128)S(1)}, f32[8]{0:T(128)}, s32[1]{0:T(128)}) custom-call(f32[8,32,512]{2,1,0:T(8,128)} %start_hbm.1, f32[8,32,512]{2,1,0:T(8,128)} %mass_hbm.1, s32[8,32,512]{2,1,0:T(8,128)} %survive_hbm.1, s32[8]{0:T(128)} %exit_hbm.1, f32[8]{0:T(128)} %demand_hbm.1, f32[32,32]{1,0:T(8,128)} %trans_hbm.1, ...), custom_call_target="tpu_custom_call" | custom-call | tf_op jit(solution)/shard_map/pallas_call | solution.py:548
  26.7 0.2 conditional.1
  27.0 0.8 %copy.61 = f32[8,32,512]{2,1,0:T(8,128)} copy(f32[8,32,512]{2,1,0:T(8,128)S(1)} %get-tuple-element.478) | data formatting | bytes 1048576
  27.8 1.1 %copy.62 = f32[8]{0:T(128)} copy(f32[8]{0:T(128)} %get-tuple-element.479) | data formatting | bytes 64
where the time goes:
time: 29.1 us; the launch traced here: 28.9 us
  Pallas kernels  25.4 us (87%)
  local copies, waits for them, and re-layouts  1.9 us (7%)
  between operations  1.34 us (5%)
    pallas_call x1, Pallas kernels, pruned_sweeps(): pl.pallas_call(functools.partial(sweeps_kernel, n_sec, n_cap), out_shape=...  25.4 us
    unnamed x2, local copies, waits for them, and re-layouts  1.9 us

commit v1 on v0

--- a/solution.py
+++ b/solution.py
@@ -11,7 +11,8 @@
 SWEEPS = 2
 CHUNK_SLOTS = 8
 SLOTS = 16
-MERGED = 16
+MERGED = 12
+UNROLLED_DEVICES = 64
 RANGES = 4
 MERGED_RANGES = 2
 NEG = -1e30
@@ -128,7 +129,7 @@
 def sweeps_kernel(n_sec, n_cap, start_hbm, mass_hbm, survive_hbm, exit_hbm, demand_hbm, trans_hbm, cost_hbm,
                   out_ref, cand_ref, rel_ref, flag_ref,
                   start_v, mass_v, survive_v, exit_v, demand_v, trans_v, cost_v,
-                  nat_ref, val_ref, live_ref, g_ref, suf_ref, best_ref, col_ref, qt_ref,
+                  nat_ref, fresh_ref, val_ref, live_ref, g_ref, suf_ref, best_ref, col_ref, qt_ref,
                   weight_ref, ones_ref, tot_ref, l1_ref, pick_ref, zsum_ref, price_ref,
                   msg_ref, gat_ref, dem_ref, dems_ref, flg_ref, flgs_ref, pay_ref, pays_ref, size_ref,
                   in_sem, msg_send, msg_recv, dem_send, dem_recv, flg_send, flg_recv, pay_send, pay_recv):
@@ -147,16 +148,27 @@
     mesh_id = pl.DeviceIdType.MESH
     f32 = jnp.float32
 
-    def device(index):
-        return {"sector": index // n_cap, "cap": lax.rem(index, n_cap)}
+    def each_other(act):
+        if n_dev > UNROLLED_DEVICES:
+            def one(off, carry):
+                index = lax.rem(me + off, n_dev)
+                act({"sector": index // n_cap, "cap": lax.rem(index, n_cap)})
+                return carry
+
+            lax.fori_loop(1, n_dev, one, 0)
+            return
+        upper = me_sec * 2 // n_sec
+        skip = me_sec + upper * (n_sec - 1 - 2 * me_sec)
+        for j in range(n_sec - 1):
+            spot = n_sec - 1 - j - (j + 1 + skip) // n_sec
+            other = spot + upper * (n_sec - 1 - 2 * spot)
+            for c in range(n_cap):
+                act({"sector": other, "cap": lax.rem(me_cap + c, n_cap)})
+        for c in range(1, n_cap):
+            act({"sector": me_sec, "cap": lax.rem(me_cap + c, n_cap)})
 
     barrier = pltpu.get_barrier_semaphore()
-
-    def greet(off, carry):
-        pl.semaphore_signal(barrier, inc=1, device_id=device(lax.rem(me + off, n_dev)), device_id_type=mesh_id)
-        return carry
-
-    lax.fori_loop(1, n_dev, greet, 0)
+    each_other(lambda device: pl.semaphore_signal(barrier, inc=1, device_id=device, device_id_type=mesh_id))
     loads = []
     for at, (src, dst) in enumerate((
         (trans_hbm, trans_v), (cost_hbm, cost_v), (exit_hbm, exit_v), (demand_hbm, demand_v),
@@ -196,7 +208,7 @@
     big_r = lax.broadcasted_iota(jnp.int32, (128, 128), 0)
     big_c = lax.broadcasted_iota(jnp.int32, (128, 128), 1)
     same = big_r // prods == big_c // prods
-    ones_ref[...] = jnp.where(same, 1.0, 0.0)
+    ones_ref[...] = jnp.where(same, 1.0, 0.0).astype(jnp.bfloat16)
 
     loads[0].wait()
     spot_r = lax.broadcasted_iota(jnp.int32, (128, prods), 0)
@@ -222,7 +234,7 @@
         col_ref[GADD, rows, :] = 0.8 * col_ref[CAP, rows, :] - nat_ref[0, pl.ds(i, 8, stride=steps), :]
         return carry
 
-    lax.fori_loop(0, steps, add_step, 0, unroll=4)
+    lax.fori_loop(0, steps, add_step, 0, unroll=8)
 
     loads[2].wait()
     loads[3].wait()
@@ -245,46 +257,37 @@
             block = jnp.where(survive_v[secs, :, at:at + 128] == 1, mass_v[secs, :, at:at + 128], 0.0)
             nat_ref[t, at:at + 128, :] = block.reshape(128, 128).T
 
-    for t in range(tiles):
-        def live_step(i, carry, t=t):
-            live_ref[t, rows_of(i), :] = jnp.where(exit_rows[t], nat_ref[t, pl.ds(i, 8, stride=steps), :], 0.0)
-            return carry
-
-        lax.fori_loop(0, steps, live_step, 0, unroll=4)
     loads[6].wait()
     for t in range(tiles):
         secs = slice(t * tile_sec, (t + 1) * tile_sec)
         for at in range(0, cap_dev, 128):
-            nat_ref[t, at:at + 128, :] = start_v[secs, :, at:at + 128].reshape(128, 128).T
-
-    def weigh(t, rows, value):
+            fresh_ref[t, at:at + 128, :] = start_v[secs, :, at:at + 128].reshape(128, 128).T
+
+    def weigh(mass, rows, value):
         scrap = 0.3 * col_ref[CAP, rows, :]
         stay = 1.0 / (1.0 + jnp.exp(2.0 * (scrap - value)))
-        return live_ref[t, rows, :] * stay * col_ref[POW, rows, :]
+        return mass * stay * col_ref[POW, rows, :]
 
     def send_supply(sweep, sums):
-        grouped = jnp.dot(
-            jnp.concatenate([part * prod_row for part in sums], axis=0), ones_ref[...],
-            precision=lax.Precision.HIGHEST, preferred_element_type=f32)
-        zsum_ref[...] = grouped
+        part = jnp.concatenate([one * prod_row for one in sums], axis=0)
+        splits = []
+        for _ in range(3):
+            splits.append(part.astype(jnp.bfloat16).astype(f32))
+            part = part - splits[-1]
+        grouped = jnp.dot(jnp.concatenate(splits, axis=0).astype(jnp.bfloat16), ones_ref[...],
+                          preferred_element_type=f32)
+        zsum_ref[...] = grouped[0:tiles * 8] + grouped[tiles * 8:tiles * 16] + grouped[tiles * 16:]
         for t in range(tiles):
             line = zsum_ref[t * 8:t * 8 + 1, :]
             for a in range(1, 8):
                 line = line + zsum_ref[t * 8 + a:t * 8 + a + 1, :]
             msg_ref[sweep, :, t * 128:(t + 1) * 128] = line
 
-        def post(off, carry):
-            message(sweep, off).start()
-            return carry
-
-        lax.fori_loop(1, n_dev, post, 0)
-        gat_ref[sweep, pl.ds(my_row, 1), :] = msg_ref[sweep]
-
-    def message(sweep, off):
-        return pltpu.make_async_remote_copy(
+        each_other(lambda device: pltpu.make_async_remote_copy(
             src_ref=msg_ref.at[sweep], dst_ref=gat_ref.at[sweep, pl.ds(my_row, 1), :],
             send_sem=msg_send.at[sweep], recv_sem=msg_recv.at[sweep],
-            device_id=device(lax.rem(me + off, n_dev)), device_id_type=mesh_id)
+            device_id=device, device_id_type=mesh_id).start())
+        gat_ref[sweep, pl.ds(my_row, 1), :] = msg_ref[sweep]
 
     def wait_rows(count, width, sem):
         view = size_ref.at[pl.ds(0, count), :, pl.ds(0, width)]
@@ -302,22 +305,17 @@
         return price_ref[pl.ds(me_sec, 1), :] / (mean * mean)
 
     def forward(t):
-        def chunk(at, carry):
-            rows = pl.ds(pl.multiple_of(at * 128, 128), 128)
-            cont = jnp.maximum(val_ref[t, rows, :], 0.3 * col_ref[CAP, rows, :])
-            upper = cont.astype(jnp.bfloat16)
-            lower = (cont - upper.astype(f32)).astype(jnp.bfloat16)
-            both = jnp.dot(jnp.concatenate([upper, lower], axis=1), weight_ref[...], preferred_element_type=f32)
-            g_ref[t, rows, :] = both[:, 0:128] + both[:, 128:256] + col_ref[GADD, rows, :]
-            return carry
-
-        lax.fori_loop(0, col_tiles, chunk, 0)
+        cont = jnp.maximum(val_ref[t], 0.3 * col_ref[CAP])
+        upper = cont.astype(jnp.bfloat16)
+        lower = (cont - upper.astype(f32)).astype(jnp.bfloat16)
+        both = jnp.dot(jnp.concatenate([upper, lower], axis=1), weight_ref[...], preferred_element_type=f32)
+        g_ref[t] = both[:, 0:128] + both[:, 128:256] + col_ref[GADD]
 
     def collect(rows_list, rank_rows, count):
-        picks = [jnp.full((8, 128), NEG, f32) for _ in range(count // 8)]
-        squares = [jnp.zeros((8, 128), f32) for _ in range(count // 8)]
+        picks = [jnp.full((8, 128), NEG, f32) for _ in range(-(-count // 8))]
+        squares = [jnp.zeros((8, 128), f32) for _ in range(-(-count // 8))]
         for (gain, square), rank in zip(rows_list, rank_rows):
-            for h in range(count // 8):
+            for h in range(-(-count // 8)):
                 here = rank == subf + 8.0 * h
                 picks[h] = jnp.where(here, gain, picks[h])
                 squares[h] = jnp.where(here, square, squares[h])
@@ -333,7 +331,7 @@
                 suf_ref[e, rows, :] = runs[e + 1]
             return tuple(jnp.maximum(run, point) for run, point in zip(runs, points))
 
-        runs = lax.fori_loop(0, steps, back, (jnp.full((8, 128), NEG, f32),) * (RANGES + 1), unroll=4)
+        runs = lax.fori_loop(0, steps, back, (jnp.full((8, 128), NEG, f32),) * (RANGES + 1), unroll=16)
         for e in range(RANGES + 1):
             tot_ref[e] = runs[e]
         before, after = bases(tot_ref, RANGES + 1, sub, 0, 7)
@@ -352,7 +350,7 @@
 
         zero = jnp.zeros((8, 128), f32)
         runs, counts, gains, squares = lax.fori_loop(
-            0, steps, ahead, (tuple(before), zero, (zero,) * CHUNK_SLOTS, (zero,) * CHUNK_SLOTS), unroll=4)
+            0, steps, ahead, (tuple(before), zero, (zero,) * CHUNK_SLOTS, (zero,) * CHUNK_SLOTS), unroll=8)
         base = counts_before(tot_ref, counts, sub)
         for p in range(CHUNK_SLOTS):
             l1_ref[0, p * 8:(p + 1) * 8, :] = gains[p]
@@ -420,7 +418,7 @@
             [(pays_ref[sweep, t, 0, a * hops + i:a * hops + i + 1, :],
               pays_ref[sweep, t, 1, a * hops + i:a * hops + i + 1, :]) for i, a in spots],
             [pick_ref[0, i * 8 + a:i * 8 + a + 1, :] for i, a in spots], MERGED)
-        for h in range(MERGED // 8):
+        for h in range(-(-MERGED // 8)):
             pick_ref[1, h * 8:(h + 1) * 8, :] = picks[h]
             pick_ref[2, h * 8:(h + 1) * 8, :] = squares[h]
         return jnp.where(base + counts > MERGED, 1.0, 0.0)
@@ -437,18 +435,20 @@
             best_ref[t, rows, :] = jnp.maximum(moved - 1.41 * capital, g_ref[t, rows, :] - 0.91 * capital)
             return carry
 
-        lax.fori_loop(0, steps, one, 0, unroll=4)
+        lax.fori_loop(0, steps, one, 0, unroll=8)
 
     sums = []
     for t in range(tiles):
         def open_step(i, acc, t=t):
             rows = rows_of(i)
-            value = jnp.where(live_ref[t, rows, :] > 0.0, nat_ref[t, pl.ds(i, 8, stride=steps), :],
-                              0.3 * col_ref[CAP, rows, :])
+            spots = pl.ds(i, 8, stride=steps)
+            mass = jnp.where(exit_rows[t], nat_ref[t, spots, :], 0.0)
+            live_ref[t, rows, :] = mass
+            value = jnp.where(mass > 0.0, fresh_ref[t, spots, :], 0.3 * col_ref[CAP, rows, :])
             val_ref[t, rows, :] = value
-            return acc + weigh(t, rows, value)
-
-        sums.append(lax.fori_loop(0, steps, open_step, jnp.zeros((8, 128), f32), unroll=8))
+            return acc + weigh(mass, rows, value)
+
+        sums.append(lax.fori_loop(0, steps, open_step, jnp.zeros((8, 128), f32), unroll=16))
     pl.semaphore_wait(barrier, n_dev - 1)
     dem_copies = []
     for off in range(1, n_sec):
@@ -473,13 +473,9 @@
         if sweep == SWEEPS - 1:
             flg_ref[...] = flag_row(flags)
 
-            def report(off, carry):
-                pltpu.make_async_remote_copy(
-                    src_ref=flg_ref, dst_ref=flgs_ref.at[pl.ds(my_row, 1), :], send_sem=flg_send, recv_sem=flg_recv,
-                    device_id=device(lax.rem(me + off, n_dev)), device_id_type=mesh_id).start()
-                return carry
-
-            lax.fori_loop(1, n_dev, report, 0)
+            each_other(lambda device: pltpu.make_async_remote_copy(
+                src_ref=flg_ref, dst_ref=flgs_ref.at[pl.ds(my_row, 1), :], send_sem=flg_send, recv_sem=flg_recv,
+                device_id=device, device_id_type=mesh_id).start())
             flgs_ref[pl.ds(my_row, 1), :] = flg_ref[...]
         late = jnp.zeros((8, 128), f32)
         for t in range(tiles):
@@ -496,29 +492,26 @@
 
                 def next_step(i, acc, t=t, scale=scale):
                     rows = rows_of(i)
-                    value = jnp.where(live_ref[t, rows, :] > 0.0,
+                    mass = live_ref[t, rows, :]
+                    value = jnp.where(mass > 0.0,
                                       scale * col_ref[POW, rows, :] + best_ref[t, rows, :],
                                       0.3 * col_ref[CAP, rows, :])
                     val_ref[t, rows, :] = value
-                    return acc + weigh(t, rows, value)
-
-                sums.append(lax.fori_loop(0, steps, next_step, jnp.zeros((8, 128), f32), unroll=8))
-    for s in range(sec_dev):
-        rel_ref[s] = relative[0, s * prods]
+                    return acc + weigh(mass, rows, value)
+
+                sums.append(lax.fori_loop(0, steps, next_step, jnp.zeros((8, 128), f32), unroll=16))
+    rel_ref[...] = relative
     for t in range(tiles):
         scale = relative[:, t * 128:(t + 1) * 128] * prod_row
 
         def last_step(i, carry, t=t, scale=scale):
             rows = rows_of(i)
-            nat_ref[t, pl.ds(i, 8, stride=steps), :] = jnp.where(
+            out_ref[t, pl.ds(i, 8, stride=steps), :] = jnp.where(
                 live_ref[t, rows, :] > 0.0, scale * col_ref[POW, rows, :] + best_ref[t, rows, :],
                 0.3 * col_ref[CAP, rows, :])
             return carry
 
         lax.fori_loop(0, steps, last_step, 0, unroll=8)
-        secs = slice(t * tile_sec, (t + 1) * tile_sec)
-        for at in range(0, cap_dev, 128):
-            out_ref[secs, :, at:at + 128] = nat_ref[t, at:at + 128, :].T.reshape(tile_sec, prods, 128)
     cand_ref[...] = pays_ref[SWEEPS - 1]
     wait_rows(n_dev - 1, 128, flg_recv)
     bad = jnp.max(jnp.maximum(jnp.max(flgs_ref[...], axis=0, keepdims=True),
@@ -548,13 +541,13 @@
     return pl.pallas_call(
         functools.partial(sweeps_kernel, n_sec, n_cap),
         out_shape=(
-            jax.ShapeDtypeStruct(start_value.shape, f32),
+            jax.ShapeDtypeStruct((tiles, cap_dev, 128), f32),
             jax.ShapeDtypeStruct((tiles, 2, n_cap * SLOTS, 128), f32),
-            jax.ShapeDtypeStruct((sec_dev,), f32),
+            jax.ShapeDtypeStruct((1, lanes), f32),
             jax.ShapeDtypeStruct((1,), jnp.int32),
         ),
         in_specs=[far] * 7,
-        out_specs=(vmem, vmem, smem, smem),
+        out_specs=(vmem, vmem, vmem, smem),
         scratch_shapes=[
             pltpu.VMEM(start_value.shape, f32),
             pltpu.VMEM(start_value.shape, f32),
@@ -567,12 +560,13 @@
             pltpu.VMEM((tiles, cap_dev, 128), f32),
             pltpu.VMEM((tiles, cap_dev, 128), f32),
             pltpu.VMEM((tiles, cap_dev, 128), f32),
+            pltpu.VMEM((tiles, cap_dev, 128), f32),
             pltpu.VMEM((pack, max(cap_dev, n_cap * SLOTS), 128), f32),
             pltpu.VMEM((tiles, cap_dev, 128), f32),
             pltpu.VMEM((5, cap_dev, 128), f32),
             pltpu.VMEM((RANGES + 1, cap_dev, 128), f32),
             pltpu.VMEM((256, 256), jnp.bfloat16),
-            pltpu.VMEM((128, 128), f32),
+            pltpu.VMEM((128, 128), jnp.bfloat16),
             pltpu.VMEM((pack + 1, 8, 128), f32),
             pltpu.VMEM((3, CHUNK_SLOTS * 8, 128), f32),
             pltpu.VMEM((3, max(MERGED, n_cap * SLOTS), 128), f32),
@@ -614,21 +608,53 @@
     return jnp.where(live, jnp.maximum(values, again), values)
 
 
+def finish_kernel(flipped_ref, row_ref, out_ref, rel_ref):
+    tile_sec, prods, cap_dev = out_ref.shape
+    lanes, sec_dev = row_ref.shape[1], rel_ref.shape[1]
+    for at in range(0, cap_dev, 128):
+        out_ref[:, :, at:at + 128] = flipped_ref[0, at:at + 128, :].T.reshape(tile_sec, prods, 128)
+
+    @pl.when(pl.program_id(0) == 0)
+    def _():
+        column = jnp.sum(jnp.where(
+            lax.broadcasted_iota(jnp.int32, (sec_dev, lanes), 1) == prods * lax.broadcasted_iota(
+                jnp.int32, (sec_dev, lanes), 0), row_ref[...], 0.0), axis=1, keepdims=True)
+        spot = lax.broadcasted_iota(jnp.int32, (sec_dev, sec_dev), 0) == lax.broadcasted_iota(
+            jnp.int32, (sec_dev, sec_dev), 1)
+        rel_ref[...] = jnp.sum(jnp.where(spot, column, 0.0), axis=0, keepdims=True)
+
+
+def finish(flipped, row, sec_dev, prods):
+    tiles, cap_dev, _ = flipped.shape
+    values, relative = pl.pallas_call(
+        finish_kernel,
+        grid=(tiles,),
+        out_shape=(jax.ShapeDtypeStruct((sec_dev, prods, cap_dev), jnp.float32),
+                   jax.ShapeDtypeStruct((1, sec_dev), jnp.float32)),
+        in_specs=[pl.BlockSpec((1, cap_dev, 128), lambda t: (t, 0, 0)),
+                  pl.BlockSpec(row.shape, lambda t: (0, 0))],
+        out_specs=(pl.BlockSpec((sec_dev // tiles, prods, cap_dev), lambda t: (t, 0, 0)),
+                   pl.BlockSpec((1, sec_dev), lambda t: (0, 0))),
+    )(flipped, row)
+    return values, relative[0]
+
+
 def on_device(start_value, firm_mass, survive, exit_index, demand, transition, install_cost):
     args = (start_value, firm_mass, survive, exit_index, demand, transition, install_cost)
     sec_dev, prods, cap_dev = start_value.shape
     if 128 % prods or prods % 8 or sec_dev * prods % 128 or cap_dev % 128 or min(
             lax.axis_size("sector"), lax.axis_size("cap")) < 2:
         return dense_sweeps(*args)
-    values, candidates, relative, state = pruned_sweeps(*args)
-    return lax.switch(
-        state[0],
-        (
-            lambda: (values, relative),
-            lambda: (all_candidates(values, candidates, relative, survive, exit_index), relative),
-            lambda: dense_sweeps(*args),
-        ),
-    )
+    flipped, candidates, row, state = pruned_sweeps(*args)
+
+    def plain():
+        return finish(flipped, row, sec_dev, prods)
+
+    def wide():
+        values, relative = plain()
+        return all_candidates(values, candidates, relative, survive, exit_index), relative
+
+    return lax.switch(state[0], (plain, wide, lambda: dense_sweeps(*args)))
 
 
 def solution(mesh):

time: 29.1 us -> 24 us (0.82)
  Pallas kernels: 25.4 us -> 22.5 us
  local copies, waits for them, and re-layouts: 1.9 us -> 0 us
    pallas_call x1, Pallas kernels: 25.4 us -> 21.4 us  [pruned_sweeps(): pl.pallas_call(functools.partial(sweeps_kernel, n_sec, n_cap), out_shape=...]
    unnamed x2 -> x0, local copies, waits for them, and re-layouts: 1.9 us -> none
    pallas_call x0 -> x1, Pallas kernels: none -> 1.04 us  [finish(): pl.pallas_call(finish_kernel, grid=(tiles,), out_shape=(jax.ShapeDtypeStr...]
where the time goes in v1:
time: 24 us; the launch traced here: 23.7 us
  Pallas kernels  22.5 us (94%)
  between operations  1.25 us (5%)
    pallas_call x1, Pallas kernels, pruned_sweeps(): pl.pallas_call(functools.partial(sweeps_kernel, n_sec, n_cap), out_shape=...  21.4 us
    pallas_call x1, Pallas kernels, finish(): pl.pallas_call(finish_kernel, grid=(tiles,), out_shape=(jax.ShapeDtypeStr...  1.04 us

profile of v1, /device:TPU:0, one launch (start us, length us, event | category | flops | bytes accessed | tf_op | source)
XLA Modules:
  0.0 23.7 jit_solution(8663888954159244635)
XLA Ops:
  0.6 21.4 %shard_map.89 = (f32[2,512,128]{2,1,0:T(8,128)S(1)}, f32[2,2,64,128]{3,2,1,0:T(8,128)S(1)}, f32[1,256]{1,0:T(1,128)S(1)}, s32[1]{0:T(128)}) custom-call(f32[8,32,512]{2,1,0:T(8,128)} %start_hbm.1, f32[8,32,512]{2,1,0:T(8,128)} %mass_hbm.1, s32[8,32,512]{2,1,0:T(8,128)} %survive_hbm.1, s32[8]{0:T(128)} %exit_hbm.1, f32[8]{0:T(128)} %demand_hbm.1, ...), custom_call_target="tpu_custom_call" | custom-call | tf_op jit(solution)/shard_map/pallas_call | solution.py:541
  22.7 1.1 %conditional.1 = (f32[8,32,512]{2,1,0:T(8,128)}, f32[8]{0:T(128)}) conditional(s32[]{:T(128)} %bitcast.49, (f32[2,512,128]{2,1,0:T(8,128)S(1)}, f32[1,256]{1,0:T(1,128)S(1)}) %tuple.56, (s32[8,32,512]{2,1,0:T(8,128)}, s32[8]{0:T(128)}, f32[2,512,128]{2,1,0:T(8,128)S(1)}, f32[1,256]{1,0:T(1,128)S(1)}, ...), branch_computations={%region_0.0_spmd, %region_1.4_spmd, %region_4.20_spmd} | conditional | flops 191131504 | bytes 93263816 | solution.py:657
  22.7 1.0 %branch_0_fun.1 = (f32[8,32,512]{2,1,0:T(8,128)}, f32[1,8]{1,0:T(1,128)}) custom-call(f32[2,512,128]{2,1,0:T(8,128)S(1)} %get-tuple-element.189.flipped_ref, f32[1,256]{1,0:T(1,128)S(1)} %get-tuple-element.190.row_ref), custom_call_target="tpu_custom_call" | custom-call | tf_op jit(solution)/shard_map/cond/branch_0_fun/pallas_call | solution.py:629

commit v2 on v1

--- a/solution.py
+++ b/solution.py
@@ -127,15 +127,16 @@
 
 
 def sweeps_kernel(n_sec, n_cap, start_hbm, mass_hbm, survive_hbm, exit_hbm, demand_hbm, trans_hbm, cost_hbm,
-                  out_ref, cand_ref, rel_ref, flag_ref,
+                  out_ref, g_ref, cand_ref, rel_ref, flag_hbm,
                   start_v, mass_v, survive_v, exit_v, demand_v, trans_v, cost_v,
-                  nat_ref, fresh_ref, val_ref, live_ref, g_ref, suf_ref, best_ref, col_ref, qt_ref,
+                  nat_ref, fresh_ref, val_ref, live_ref, suf_ref, best_ref, col_ref, qt_ref,
                   weight_ref, ones_ref, tot_ref, l1_ref, pick_ref, zsum_ref, price_ref,
-                  msg_ref, gat_ref, dem_ref, dems_ref, flg_ref, flgs_ref, pay_ref, pays_ref, size_ref,
-                  in_sem, msg_send, msg_recv, dem_send, dem_recv, flg_send, flg_recv, pay_send, pay_recv):
+                  msg_ref, gat_ref, dem_ref, dems_ref, pay_ref, pays_ref, size_ref, flag_ref,
+                  in_sem, msg_send, msg_recv, dem_send, dem_recv, pay_send, pay_recv):
     sec_dev, prods, cap_dev = start_v.shape
     total = cap_dev * n_cap
     steps = cap_dev // 8
+    pitch = steps + 8
     tiles = sec_dev * prods // 128
     tile_sec = 128 // prods
     lanes = tiles * 128
@@ -167,8 +168,6 @@
         for c in range(1, n_cap):
             act({"sector": me_sec, "cap": lax.rem(me_cap + c, n_cap)})
 
-    barrier = pltpu.get_barrier_semaphore()
-    each_other(lambda device: pl.semaphore_signal(barrier, inc=1, device_id=device, device_id_type=mesh_id))
     loads = []
     for at, (src, dst) in enumerate((
         (trans_hbm, trans_v), (cost_hbm, cost_v), (exit_hbm, exit_v), (demand_hbm, demand_v),
@@ -177,6 +176,8 @@
         loads.append(pltpu.make_async_copy(src, dst, in_sem.at[at]))
         loads[-1].start()
 
+    barrier = pltpu.get_barrier_semaphore()
+    each_other(lambda device: pl.semaphore_signal(barrier, inc=1, device_id=device, device_id_type=mesh_id))
     sub = lax.broadcasted_iota(jnp.int32, (8, 128), 0)
     subf = sub.astype(f32)
     lane = lax.broadcasted_iota(jnp.int32, (1, 128), 1)
@@ -225,13 +226,18 @@
     weight_ref[0:128, 128:256] = low
     weight_ref[128:256, 128:256] = jnp.zeros_like(low)
 
+    def place_rows(ref, t, at, block):
+        for up in range(0, 128, steps):
+            spot = (at + up) // steps * pitch
+            ref[t, spot:spot + steps, :] = block[up:up + steps]
+
     loads[1].wait()
     for at in range(0, cap_dev, 128):
-        nat_ref[0, at:at + 128, :] = jnp.broadcast_to(cost_v[:, at:at + 128], (128, 128)).T
+        place_rows(nat_ref, 0, at, jnp.broadcast_to(cost_v[:, at:at + 128], (128, 128)).T)
 
     def add_step(i, carry):
         rows = rows_of(i)
-        col_ref[GADD, rows, :] = 0.8 * col_ref[CAP, rows, :] - nat_ref[0, pl.ds(i, 8, stride=steps), :]
+        col_ref[GADD, rows, :] = 0.8 * col_ref[CAP, rows, :] - nat_ref[0, pl.ds(i, 8, stride=pitch), :]
         return carry
 
     lax.fori_loop(0, steps, add_step, 0, unroll=8)
@@ -255,20 +261,20 @@
         secs = slice(t * tile_sec, (t + 1) * tile_sec)
         for at in range(0, cap_dev, 128):
             block = jnp.where(survive_v[secs, :, at:at + 128] == 1, mass_v[secs, :, at:at + 128], 0.0)
-            nat_ref[t, at:at + 128, :] = block.reshape(128, 128).T
+            place_rows(nat_ref, t, at, block.reshape(128, 128).T)
 
     loads[6].wait()
     for t in range(tiles):
         secs = slice(t * tile_sec, (t + 1) * tile_sec)
         for at in range(0, cap_dev, 128):
-            fresh_ref[t, at:at + 128, :] = start_v[secs, :, at:at + 128].reshape(128, 128).T
+            place_rows(fresh_ref, t, at, start_v[secs, :, at:at + 128].reshape(128, 128).T)
 
     def weigh(mass, rows, value):
         scrap = 0.3 * col_ref[CAP, rows, :]
-        stay = 1.0 / (1.0 + jnp.exp(2.0 * (scrap - value)))
+        stay = 0.5 + 0.5 * jnp.tanh(value - scrap)
         return mass * stay * col_ref[POW, rows, :]
 
-    def send_supply(sweep, sums):
+    def fold_supply(sweep, sums):
         part = jnp.concatenate([one * prod_row for one in sums], axis=0)
         splits = []
         for _ in range(3):
@@ -283,6 +289,7 @@
                 line = line + zsum_ref[t * 8 + a:t * 8 + a + 1, :]
             msg_ref[sweep, :, t * 128:(t + 1) * 128] = line
 
+    def send_supply(sweep):
         each_other(lambda device: pltpu.make_async_remote_copy(
             src_ref=msg_ref.at[sweep], dst_ref=gat_ref.at[sweep, pl.ds(my_row, 1), :],
             send_sem=msg_send.at[sweep], recv_sem=msg_recv.at[sweep],
@@ -304,12 +311,16 @@
         mean = jnp.sum(jnp.sqrt(prices), keepdims=True) / (lanes * n_sec)
         return price_ref[pl.ds(me_sec, 1), :] / (mean * mean)
 
-    def forward(t):
-        cont = jnp.maximum(val_ref[t], 0.3 * col_ref[CAP])
-        upper = cont.astype(jnp.bfloat16)
-        lower = (cont - upper.astype(f32)).astype(jnp.bfloat16)
-        both = jnp.dot(jnp.concatenate([upper, lower], axis=1), weight_ref[...], preferred_element_type=f32)
-        g_ref[t] = both[:, 0:128] + both[:, 128:256] + col_ref[GADD]
+    def forward():
+        halves = []
+        for t in range(tiles):
+            cont = jnp.maximum(val_ref[t], 0.3 * col_ref[CAP])
+            upper = cont.astype(jnp.bfloat16)
+            halves.append(jnp.concatenate([upper, (cont - upper.astype(f32)).astype(jnp.bfloat16)], axis=1))
+        both = jnp.dot(jnp.concatenate(halves, axis=0), weight_ref[...], preferred_element_type=f32)
+        for t in range(tiles):
+            rows = slice(t * cap_dev, (t + 1) * cap_dev)
+            g_ref[t] = both[rows, 0:128] + both[rows, 128:256] + col_ref[GADD]
 
     def collect(rows_list, rank_rows, count):
         picks = [jnp.full((8, 128), NEG, f32) for _ in range(-(-count // 8))]
@@ -360,14 +371,20 @@
         picks, squares = collect(
             [(l1_ref[0, r:r + 1, :], l1_ref[1, r:r + 1, :]) for r in spots],
             [l1_ref[2, r:r + 1, :] for r in spots], SLOTS)
-        mine = pl.ds(pl.multiple_of(me_cap * SLOTS, SLOTS), SLOTS)
+        over = flag_row(jnp.where((counts > CHUNK_SLOTS) | (base + counts > SLOTS), 1.0, 0.0))
         for h in range(SLOTS // 8):
             pay_ref[sweep, t, 0, h * 8:(h + 1) * 8, :] = picks[h]
-            pay_ref[sweep, t, 1, h * 8:(h + 1) * 8, :] = squares[h]
+            pay_ref[sweep, t, 1, h * 8:(h + 1) * 8, :] = jnp.where(over > 0.0, -1.0, squares[h])
+
+    def send_payment(sweep, t):
+        mine = pl.ds(pl.multiple_of(me_cap * SLOTS, SLOTS), SLOTS)
         for off in range(1, n_cap):
             payment(sweep, t, off).start()
         pays_ref[sweep, t, :, mine, :] = pay_ref[sweep, t]
-        return jnp.where((counts > CHUNK_SLOTS) | (base + counts > SLOTS), 1.0, 0.0)
+
+    def flag_row(flags):
+        tot_ref[0] = flags
+        return all_max([tot_ref[0, a:a + 1, :] for a in range(8)])
 
     def payment(sweep, t, off):
         mine = pl.ds(pl.multiple_of(me_cap * SLOTS, SLOTS), SLOTS)
@@ -401,15 +418,16 @@
         before, after = bases(tot_ref, MERGED_RANGES + 1, sub, 0, 7)
 
         def ahead(i, carry):
-            runs, counts = carry
+            runs, counts, lost = carry
             gain, square = line(i)
             points = [gain - square * near[e] for e in range(MERGED_RANGES + 1)]
             keep = useful(points, runs, [suf_ref[e, rows_of(i), :] for e in range(MERGED_RANGES)], after)
             runs = tuple(jnp.maximum(run, point) for run, point in zip(runs, points))
             pick_ref[0, rows_of(i), :] = jnp.where(keep, counts, NEG)
-            return runs, counts + jnp.where(keep, 1.0, 0.0)
-
-        runs, counts = lax.fori_loop(0, hops, ahead, (tuple(before), jnp.zeros((8, 128), f32)), unroll=8)
+            return runs, counts + jnp.where(keep, 1.0, 0.0), jnp.minimum(lost, square)
+
+        zero = jnp.zeros((8, 128), f32)
+        runs, counts, lost = lax.fori_loop(0, hops, ahead, (tuple(before), zero, zero), unroll=8)
         base = counts_before(tot_ref, counts, sub)
         for i in range(hops):
             pick_ref[0, i * 8:(i + 1) * 8, :] = pick_ref[0, i * 8:(i + 1) * 8, :] + base
@@ -421,7 +439,7 @@
         for h in range(-(-MERGED // 8)):
             pick_ref[1, h * 8:(h + 1) * 8, :] = picks[h]
             pick_ref[2, h * 8:(h + 1) * 8, :] = squares[h]
-        return jnp.where(base + counts > MERGED, 1.0, 0.0)
+        return jnp.where(lost < 0.0, 2.0, jnp.where(base + counts > MERGED, 1.0, 0.0))
 
     def reply(t):
         gains = [jnp.broadcast_to(pick_ref[1, c:c + 1, :], (8, 128)) for c in range(MERGED)]
@@ -441,7 +459,7 @@
     for t in range(tiles):
         def open_step(i, acc, t=t):
             rows = rows_of(i)
-            spots = pl.ds(i, 8, stride=steps)
+            spots = pl.ds(i, 8, stride=pitch)
             mass = jnp.where(exit_rows[t], nat_ref[t, spots, :], 0.0)
             live_ref[t, rows, :] = mass
             value = jnp.where(mass > 0.0, fresh_ref[t, spots, :], 0.3 * col_ref[CAP, rows, :])
@@ -449,40 +467,31 @@
             return acc + weigh(mass, rows, value)
 
         sums.append(lax.fori_loop(0, steps, open_step, jnp.zeros((8, 128), f32), unroll=16))
-    pl.semaphore_wait(barrier, n_dev - 1)
-    dem_copies = []
-    for off in range(1, n_sec):
-        dem_copies.append(pltpu.make_async_remote_copy(
-            src_ref=dem_ref, dst_ref=dems_ref.at[pl.ds(me_sec, 1), :], send_sem=dem_send, recv_sem=dem_recv,
-            device_id={"sector": lax.rem(me_sec + off, n_sec)}, device_id_type=mesh_id))
-        dem_copies[-1].start()
+    msg_ref[0, :, lanes:lanes + 128] = jnp.zeros((1, 128), f32)
+    dem_copies = [pltpu.make_async_remote_copy(
+        src_ref=dem_ref, dst_ref=dems_ref.at[pl.ds(me_sec, 1), :], send_sem=dem_send, recv_sem=dem_recv,
+        device_id={"sector": lax.rem(me_sec + off, n_sec)}, device_id_type=mesh_id) for off in range(1, n_sec)]
     dems_ref[pl.ds(me_sec, 1), :] = dem_ref[...]
-    msg_ref[0, :, lanes:lanes + 128] = jnp.zeros((1, 128), f32)
-
-    def flag_row(flags):
-        tot_ref[0] = flags
-        return all_max([tot_ref[0, a:a + 1, :] for a in range(8)])
-
-    late = None
+    state = jnp.zeros((8, 128), f32)
     for sweep in range(SWEEPS):
-        send_supply(sweep, sums)
-        flags = jnp.zeros((8, 128), f32)
+        fold_supply(sweep, sums)
+        if sweep > 0:
+            send_supply(sweep)
+        forward()
         for t in range(tiles):
-            forward(t)
-            flags = jnp.maximum(flags, prune(sweep, t))
-        if sweep == SWEEPS - 1:
-            flg_ref[...] = flag_row(flags)
-
-            each_other(lambda device: pltpu.make_async_remote_copy(
-                src_ref=flg_ref, dst_ref=flgs_ref.at[pl.ds(my_row, 1), :], send_sem=flg_send, recv_sem=flg_recv,
-                device_id=device, device_id_type=mesh_id).start())
-            flgs_ref[pl.ds(my_row, 1), :] = flg_ref[...]
-        late = jnp.zeros((8, 128), f32)
+            prune(sweep, t)
+            if sweep == 0 and t == 0:
+                pl.semaphore_wait(barrier, n_dev - 1)
+                send_supply(sweep)
+                for copy in dem_copies:
+                    copy.start()
+            send_payment(sweep, t)
         for t in range(tiles):
-            late = jnp.maximum(late, merge(sweep, t))
+            state = jnp.maximum(state, merge(sweep, t))
             reply(t)
         if sweep == 0:
-            msg_ref[1, :, lanes:lanes + 128] = flag_row(jnp.maximum(flags, late))
+            msg_ref[1, :, lanes:lanes + 128] = flag_row(state)
+            state = jnp.zeros((8, 128), f32)
             wait_rows(n_sec - 1, lanes, dem_recv)
         relative = prices_row(sweep)
         if sweep == 0:
@@ -501,29 +510,28 @@
 
                 sums.append(lax.fori_loop(0, steps, next_step, jnp.zeros((8, 128), f32), unroll=16))
     rel_ref[...] = relative
+    early = jnp.max(gat_ref[1, :, lanes:lanes + 128], axis=0, keepdims=True)
+    flag_ref[0] = jnp.max(jnp.maximum(state, jnp.where(early > 0.0, 3.0, 0.0))).astype(jnp.int32)
+    report = pltpu.make_async_copy(flag_ref, flag_hbm, in_sem.at[0])
+    report.start()
     for t in range(tiles):
         scale = relative[:, t * 128:(t + 1) * 128] * prod_row
 
         def last_step(i, carry, t=t, scale=scale):
             rows = rows_of(i)
-            out_ref[t, pl.ds(i, 8, stride=steps), :] = jnp.where(
+            out_ref[t, pl.ds(i, 8, stride=pitch), :] = jnp.where(
                 live_ref[t, rows, :] > 0.0, scale * col_ref[POW, rows, :] + best_ref[t, rows, :],
                 0.3 * col_ref[CAP, rows, :])
             return carry
 
         lax.fori_loop(0, steps, last_step, 0, unroll=8)
     cand_ref[...] = pays_ref[SWEEPS - 1]
-    wait_rows(n_dev - 1, 128, flg_recv)
-    bad = jnp.max(jnp.maximum(jnp.max(flgs_ref[...], axis=0, keepdims=True),
-                              jnp.max(gat_ref[1, :, lanes:lanes + 128], axis=0, keepdims=True)))
-    flag_ref[0] = jnp.where(bad > 0.0, 2, jnp.where(jnp.max(late) > 0.0, 1, 0)).astype(jnp.int32)
-
     for sweep in range(SWEEPS):
         wait_rows(n_dev - 1, lanes + 128, msg_send.at[sweep])
         for t in range(tiles):
             pltpu.make_async_copy(pay_view(sweep, t), pay_view(sweep, t), pay_send.at[sweep, t]).wait()
-    wait_rows(n_dev - 1, 128, flg_send)
     wait_rows(n_sec - 1, lanes, dem_send)
+    report.wait()
 
 
 def pruned_sweeps(start_value, firm_mass, survive, exit_index, demand, transition, install_cost):
@@ -541,13 +549,14 @@
     return pl.pallas_call(
         functools.partial(sweeps_kernel, n_sec, n_cap),
         out_shape=(
+            jax.ShapeDtypeStruct((tiles, cap_dev + 64, 128), f32),
             jax.ShapeDtypeStruct((tiles, cap_dev, 128), f32),
             jax.ShapeDtypeStruct((tiles, 2, n_cap * SLOTS, 128), f32),
             jax.ShapeDtypeStruct((1, lanes), f32),
             jax.ShapeDtypeStruct((1,), jnp.int32),
         ),
         in_specs=[far] * 7,
-        out_specs=(vmem, vmem, vmem, smem),
+        out_specs=(vmem, vmem, vmem, vmem, far),
         scratch_shapes=[
             pltpu.VMEM(start_value.shape, f32),
             pltpu.VMEM(start_value.shape, f32),
@@ -556,9 +565,8 @@
             pltpu.SMEM((sec_dev,), f32),
             pltpu.VMEM((prods, prods), f32),
             pltpu.VMEM((1, cap_dev), f32),
-            pltpu.VMEM((tiles, cap_dev, 128), f32),
-            pltpu.VMEM((tiles, cap_dev, 128), f32),
-            pltpu.VMEM((tiles, cap_dev, 128), f32),
+            pltpu.VMEM((tiles, cap_dev + 64, 128), f32),
+            pltpu.VMEM((tiles, cap_dev + 64, 128), f32),
             pltpu.VMEM((tiles, cap_dev, 128), f32),
             pltpu.VMEM((tiles, cap_dev, 128), f32),
             pltpu.VMEM((pack, max(cap_dev, n_cap * SLOTS), 128), f32),
@@ -576,13 +584,12 @@
             pltpu.VMEM((SWEEPS, n_dev, lanes + 128), f32),
             pltpu.VMEM((1, lanes), f32),
             pltpu.VMEM((n_sec, lanes), f32),
-            pltpu.VMEM((1, 128), f32),
-            pltpu.VMEM((n_dev, 128), f32),
             pltpu.VMEM((SWEEPS, tiles, 2, SLOTS, 128), f32),
             pltpu.VMEM((SWEEPS, tiles, 2, n_cap * SLOTS, 128), f32),
             pltpu.VMEM((n_dev - 1, 1, lanes + 128), f32),
+            pltpu.SMEM((1,), jnp.int32),
             dma((7,)),
-            dma((SWEEPS,)), dma((SWEEPS,)), dma, dma, dma, dma,
+            dma((SWEEPS,)), dma((SWEEPS,)), dma, dma,
             dma((SWEEPS, tiles)), dma((SWEEPS, tiles)),
         ],
         compiler_params=pltpu.CompilerParams(
@@ -608,11 +615,30 @@
     return jnp.where(live, jnp.maximum(values, again), values)
 
 
+def group_sweep(gains, relative, survive, exit_index):
+    sec_dev, prods, cap_dev = survive.shape
+    tiles = gains.shape[0]
+    total = cap_dev * lax.axis_size("cap")
+    row_first = lax.axis_index("cap") * cap_dev
+    capital = capital_of(row_first + jnp.arange(cap_dev, dtype=jnp.int32), total)
+    prod_index = jnp.arange(prods, dtype=jnp.int32)
+    output = jnp.exp(-0.5 + prod_index.astype(jnp.float32) / (prods - 1))[:, None] * capital[None, :] ** 0.6
+    live = (survive == 1) & (prod_index[None, :, None] >= exit_index[:, None, None])
+    natural = gains.reshape(tiles, cap_dev // 8, 8, 128).swapaxes(1, 2).reshape(tiles, cap_dev, 128)
+    forward_value = natural.swapaxes(1, 2).reshape(sec_dev, prods, cap_dev) - 0.8 * capital
+    rows = jnp.moveaxis(gather_blocks(forward_value, "cap"), 0, 2).reshape(sec_dev * prods, total)
+    best = best_reply(rows, row_first, cap_dev).reshape(sec_dev, prods, cap_dev)
+    return jnp.where(live, relative[:, None, None] * output + best, 0.3 * capital)
+
+
 def finish_kernel(flipped_ref, row_ref, out_ref, rel_ref):
     tile_sec, prods, cap_dev = out_ref.shape
     lanes, sec_dev = row_ref.shape[1], rel_ref.shape[1]
+    steps = cap_dev // 8
     for at in range(0, cap_dev, 128):
-        out_ref[:, :, at:at + 128] = flipped_ref[0, at:at + 128, :].T.reshape(tile_sec, prods, 128)
+        spots = [(at + up) // steps * (steps + 8) for up in range(0, 128, steps)]
+        block = jnp.concatenate([flipped_ref[0, spot:spot + steps, :] for spot in spots], axis=0)
+        out_ref[:, :, at:at + 128] = block.T.reshape(tile_sec, prods, 128)
 
     @pl.when(pl.program_id(0) == 0)
     def _():
@@ -625,13 +651,14 @@
 
 
 def finish(flipped, row, sec_dev, prods):
-    tiles, cap_dev, _ = flipped.shape
+    tiles, padded, _ = flipped.shape
+    cap_dev = padded - 64
     values, relative = pl.pallas_call(
         finish_kernel,
         grid=(tiles,),
         out_shape=(jax.ShapeDtypeStruct((sec_dev, prods, cap_dev), jnp.float32),
                    jax.ShapeDtypeStruct((1, sec_dev), jnp.float32)),
-        in_specs=[pl.BlockSpec((1, cap_dev, 128), lambda t: (t, 0, 0)),
+        in_specs=[pl.BlockSpec((1, padded, 128), lambda t: (t, 0, 0)),
                   pl.BlockSpec(row.shape, lambda t: (0, 0))],
         out_specs=(pl.BlockSpec((sec_dev // tiles, prods, cap_dev), lambda t: (t, 0, 0)),
                    pl.BlockSpec((1, sec_dev), lambda t: (0, 0))),
@@ -645,7 +672,7 @@
     if 128 % prods or prods % 8 or sec_dev * prods % 128 or cap_dev % 128 or min(
             lax.axis_size("sector"), lax.axis_size("cap")) < 2:
         return dense_sweeps(*args)
-    flipped, candidates, row, state = pruned_sweeps(*args)
+    flipped, gains, candidates, row, state = pruned_sweeps(*args)
 
     def plain():
         return finish(flipped, row, sec_dev, prods)
@@ -654,7 +681,11 @@
         values, relative = plain()
         return all_candidates(values, candidates, relative, survive, exit_index), relative
 
-    return lax.switch(state[0], (plain, wide, lambda: dense_sweeps(*args)))
+    def group():
+        relative = row.reshape(sec_dev, prods)[:, 0]
+        return group_sweep(gains, relative, survive, exit_index), relative
+
+    return lax.switch(state[0], (plain, wide, group, lambda: dense_sweeps(*args)))
 
 
 def solution(mesh):

time: 24 us -> 22 us (0.917)
  Pallas kernels: 22.5 us -> 20.4 us
    pallas_call x1, Pallas kernels: 21.4 us -> 19.4 us  [pruned_sweeps(): pl.pallas_call(functools.partial(sweeps_kernel, n_sec, n_cap), out_shape=...]
where the time goes in v2:
time: 22 us; the launch traced here: 21.7 us
  Pallas kernels  20.4 us (93%)
  between operations  1.26 us (6%)
    pallas_call x1, Pallas kernels, pruned_sweeps(): pl.pallas_call(functools.partial(sweeps_kernel, n_sec, n_cap), out_shape=...  19.4 us
    pallas_call x1, Pallas kernels, finish(): pl.pallas_call(finish_kernel, grid=(tiles,), out_shape=(jax.ShapeDtypeStr...  1.04 us

profile of v2, /device:TPU:0, one launch (start us, length us, event | category | flops | bytes accessed | tf_op | source)
XLA Modules:
  0.0 21.7 jit_solution(3921223801639669076)
XLA Ops:
  0.6 19.4 %shard_map.90 = (f32[2,576,128]{2,1,0:T(8,128)S(1)}, f32[2,512,128]{2,1,0:T(8,128)S(1)}, f32[2,2,64,128]{3,2,1,0:T(8,128)S(1)}, f32[1,256]{1,0:T(1,128)S(1)}, s32[1]{0:T(128)}) custom-call(f32[8,32,512]{2,1,0:T(8,128)} %start_hbm.1, f32[8,32,512]{2,1,0:T(8,128)} %mass_hbm.1, s32[8,32,512]{2,1,0:T(8,128)} %survive_hbm.1, s32[8]{0:T(128)} %exit_hbm.1, ...), custom_call_target="tpu_custom_call" | custom-call | tf_op jit(solution)/shard_map/pallas_call | solution.py:549
  20.7 1.1 %conditional.1 = (f32[8,32,512]{2,1,0:T(8,128)}, f32[8]{0:T(128)}) conditional(s32[]{:T(128)} %bitcast.64, (f32[2,576,128]{2,1,0:T(8,128)S(1)}, f32[1,256]{1,0:T(1,128)S(1)}) %tuple.75, (s32[8,32,512]{2,1,0:T(8,128)}, s32[8]{0:T(128)}, f32[2,576,128]{2,1,0:T(8,128)S(1)}, f32[1,256]{1,0:T(1,128)S(1)}, ...), branch_computations={%region_0.0_spmd, %region_1.4_spmd, %region_4.9_spmd, %region_8.24... | conditional | flops 191131504 | bytes 93263816 | solution.py:688
  20.7 1.0 %branch_0_fun.1 = (f32[8,32,512]{2,1,0:T(8,128)}, f32[1,8]{1,0:T(1,128)}) custom-call(f32[2,576,128]{2,1,0:T(8,128)S(1)} %get-tuple-element.266.flipped_ref, f32[1,256]{1,0:T(1,128)S(1)} %get-tuple-element.267.row_ref), custom_call_target="tpu_custom_call" | custom-call | tf_op jit(solution)/shard_map/cond/branch_0_fun/pallas_call | solution.py:656

commit v3 on v2

--- a/solution.py
+++ b/solution.py
@@ -99,7 +99,7 @@
     return functools.reduce(jnp.maximum, parts)
 
 
-def bases(tot_ref, count, sub, first, last):
+def bases(tot_ref, count, sub):
     before, after = [], []
     for e in range(count):
         rows = [tot_ref[e, a:a + 1, :] for a in range(8)]
@@ -129,7 +129,7 @@
 def sweeps_kernel(n_sec, n_cap, start_hbm, mass_hbm, survive_hbm, exit_hbm, demand_hbm, trans_hbm, cost_hbm,
                   out_ref, g_ref, cand_ref, rel_ref, flag_hbm,
                   start_v, mass_v, survive_v, exit_v, demand_v, trans_v, cost_v,
-                  nat_ref, fresh_ref, val_ref, live_ref, suf_ref, best_ref, col_ref, qt_ref,
+                  nat_ref, fresh_ref, val_ref, live_ref, pre_ref, ends_ref, suf_ref, best_ref, col_ref, qt_ref,
                   weight_ref, ones_ref, tot_ref, l1_ref, pick_ref, zsum_ref, price_ref,
                   msg_ref, gat_ref, dem_ref, dems_ref, pay_ref, pays_ref, size_ref, flag_ref,
                   in_sem, msg_send, msg_recv, dem_send, dem_recv, pay_send, pay_recv):
@@ -149,8 +149,11 @@
     mesh_id = pl.DeviceIdType.MESH
     f32 = jnp.float32
 
-    def each_other(act):
+    def each_other(act, far=True, close=True):
         if n_dev > UNROLLED_DEVICES:
+            if not far:
+                return
+
             def one(off, carry):
                 index = lax.rem(me + off, n_dev)
                 act({"sector": index // n_cap, "cap": lax.rem(index, n_cap)})
@@ -160,12 +163,12 @@
             return
         upper = me_sec * 2 // n_sec
         skip = me_sec + upper * (n_sec - 1 - 2 * me_sec)
-        for j in range(n_sec - 1):
+        for j in range(0 if far else n_sec // 2, n_sec - 1 if close else n_sec // 2):
             spot = n_sec - 1 - j - (j + 1 + skip) // n_sec
             other = spot + upper * (n_sec - 1 - 2 * spot)
             for c in range(n_cap):
                 act({"sector": other, "cap": lax.rem(me_cap + c, n_cap)})
-        for c in range(1, n_cap):
+        for c in range(1, n_cap if close else 1):
             act({"sector": me_sec, "cap": lax.rem(me_cap + c, n_cap)})
 
     loads = []
@@ -214,13 +217,17 @@
     loads[0].wait()
     spot_r = lax.broadcasted_iota(jnp.int32, (128, prods), 0)
     spot_c = lax.broadcasted_iota(jnp.int32, (128, prods), 1)
-    spot = jnp.where(lax.rem(spot_r, prods) == spot_c, 1.0, 0.0)
-    dims = (((1,), (1,)), ((), ()))
-    half = lax.dot_general(spot, trans_v[...], dims, precision=lax.Precision.HIGHEST, preferred_element_type=f32)
-    full = lax.dot_general(half, spot, dims, precision=lax.Precision.HIGHEST, preferred_element_type=f32)
-    weight = jnp.where(same, 0.9 * full, 0.0)
-    top = weight.astype(jnp.bfloat16)
-    low = (weight - top.astype(f32)).astype(jnp.bfloat16)
+    spot = jnp.where(lax.rem(spot_r, prods) == spot_c, 1.0, 0.0).astype(jnp.bfloat16)
+    scaled = 0.9 * trans_v[...]
+    upper = scaled.astype(jnp.bfloat16)
+    pair = jnp.concatenate([upper, (scaled - upper.astype(f32)).astype(jnp.bfloat16)], axis=0)
+    half = lax.dot_general(spot, pair, (((1,), (1,)), ((), ())), preferred_element_type=f32)
+    fan_r = lax.broadcasted_iota(jnp.int32, (2 * prods, 256), 0)
+    fan_c = lax.broadcasted_iota(jnp.int32, (2 * prods, 256), 1)
+    fan = (lax.rem(fan_r, prods) == lax.rem(fan_c, prods)) & (fan_r // prods == fan_c // 128)
+    full = jnp.dot(half.astype(jnp.bfloat16), jnp.where(fan, 1.0, 0.0).astype(jnp.bfloat16), preferred_element_type=f32)
+    top = jnp.where(same, full[:, 0:128], 0.0).astype(jnp.bfloat16)
+    low = jnp.where(same, full[:, 128:256], 0.0).astype(jnp.bfloat16)
     weight_ref[0:128, 0:128] = top
     weight_ref[128:256, 0:128] = top
     weight_ref[0:128, 128:256] = low
@@ -289,12 +296,13 @@
                 line = line + zsum_ref[t * 8 + a:t * 8 + a + 1, :]
             msg_ref[sweep, :, t * 128:(t + 1) * 128] = line
 
-    def send_supply(sweep):
+    def send_supply(sweep, far, close):
         each_other(lambda device: pltpu.make_async_remote_copy(
             src_ref=msg_ref.at[sweep], dst_ref=gat_ref.at[sweep, pl.ds(my_row, 1), :],
             send_sem=msg_send.at[sweep], recv_sem=msg_recv.at[sweep],
-            device_id=device, device_id_type=mesh_id).start())
-        gat_ref[sweep, pl.ds(my_row, 1), :] = msg_ref[sweep]
+            device_id=device, device_id_type=mesh_id).start(), far, close)
+        if far:
+            gat_ref[sweep, pl.ds(my_row, 1), :] = msg_ref[sweep]
 
     def wait_rows(count, width, sem):
         view = size_ref.at[pl.ds(0, count), :, pl.ds(0, width)]
@@ -319,8 +327,16 @@
             halves.append(jnp.concatenate([upper, (cont - upper.astype(f32)).astype(jnp.bfloat16)], axis=1))
         both = jnp.dot(jnp.concatenate(halves, axis=0), weight_ref[...], preferred_element_type=f32)
         for t in range(tiles):
-            rows = slice(t * cap_dev, (t + 1) * cap_dev)
-            g_ref[t] = both[rows, 0:128] + both[rows, 128:256] + col_ref[GADD]
+            runs = [jnp.full((8, 128), NEG, f32)] * (RANGES + 1)
+            for at in range(0, cap_dev, 8):
+                rows, here = slice(at, at + 8), t * cap_dev + at
+                gain = both[here:here + 8, 0:128] + both[here:here + 8, 128:256] + col_ref[GADD, rows, :]
+                g_ref[t, rows, :] = gain
+                for e in range(RANGES):
+                    pre_ref[t, e, rows, :] = runs[e]
+                runs = [jnp.maximum(run, gain - qt_ref[e, rows, :]) for e, run in enumerate(runs)]
+            for e in range(RANGES + 1):
+                ends_ref[t, e] = runs[e]
 
     def collect(rows_list, rank_rows, count):
         picks = [jnp.full((8, 128), NEG, f32) for _ in range(-(-count // 8))]
@@ -333,40 +349,28 @@
         return picks, squares
 
     def prune(sweep, t):
-        def back(at, runs):
-            i = steps - 1 - at
-            rows = rows_of(i)
-            gain = g_ref[t, rows, :]
-            points = [gain - qt_ref[e, rows, :] for e in range(RANGES + 1)]
-            for e in range(RANGES):
-                suf_ref[e, rows, :] = runs[e + 1]
-            return tuple(jnp.maximum(run, point) for run, point in zip(runs, points))
-
-        runs = lax.fori_loop(0, steps, back, (jnp.full((8, 128), NEG, f32),) * (RANGES + 1), unroll=16)
-        for e in range(RANGES + 1):
-            tot_ref[e] = runs[e]
-        before, after = bases(tot_ref, RANGES + 1, sub, 0, 7)
-
-        def ahead(i, carry):
+        before, after = bases(ends_ref.at[t], RANGES + 1, sub)
+
+        def down(at, carry):
             runs, counts, gains, squares = carry
-            rows = rows_of(i)
+            rows = rows_of(steps - 1 - at)
             gain = g_ref[t, rows, :]
             square = col_ref[SQUARE, rows, :]
             points = [gain - qt_ref[e, rows, :] for e in range(RANGES + 1)]
-            keep = useful(points, runs, [suf_ref[e, rows, :] for e in range(RANGES)], after)
-            runs = tuple(jnp.maximum(run, point) for run, point in zip(runs, points))
+            keep = useful(points[::-1], runs, [pre_ref[t, e, rows, :] for e in range(RANGES)][::-1], before[::-1])
+            runs = tuple(jnp.maximum(run, point) for run, point in zip(runs, points[::-1]))
             gains = tuple(jnp.where(keep, new, old) for new, old in zip((gain,) + gains, gains))
             squares = tuple(jnp.where(keep, new, old) for new, old in zip((square,) + squares, squares))
             return runs, counts + jnp.where(keep, 1.0, 0.0), gains, squares
 
         zero = jnp.zeros((8, 128), f32)
         runs, counts, gains, squares = lax.fori_loop(
-            0, steps, ahead, (tuple(before), zero, (zero,) * CHUNK_SLOTS, (zero,) * CHUNK_SLOTS), unroll=8)
+            0, steps, down, (tuple(after[::-1]), zero, (zero,) * CHUNK_SLOTS, (zero,) * CHUNK_SLOTS), unroll=8)
         base = counts_before(tot_ref, counts, sub)
         for p in range(CHUNK_SLOTS):
             l1_ref[0, p * 8:(p + 1) * 8, :] = gains[p]
             l1_ref[1, p * 8:(p + 1) * 8, :] = squares[p]
-            l1_ref[2, p * 8:(p + 1) * 8, :] = jnp.where(counts > p, base + counts - (p + 1.0), -1.0)
+            l1_ref[2, p * 8:(p + 1) * 8, :] = jnp.where(counts > p, base + p, -1.0)
         spots = range(CHUNK_SLOTS * 8)
         picks, squares = collect(
             [(l1_ref[0, r:r + 1, :], l1_ref[1, r:r + 1, :]) for r in spots],
@@ -415,7 +419,7 @@
         runs = lax.fori_loop(0, hops, back, (jnp.full((8, 128), NEG, f32),) * (MERGED_RANGES + 1), unroll=8)
         for e in range(MERGED_RANGES + 1):
             tot_ref[e] = runs[e]
-        before, after = bases(tot_ref, MERGED_RANGES + 1, sub, 0, 7)
+        before, after = bases(tot_ref, MERGED_RANGES + 1, sub)
 
         def ahead(i, carry):
             runs, counts, lost = carry
@@ -475,17 +479,21 @@
     state = jnp.zeros((8, 128), f32)
     for sweep in range(SWEEPS):
         fold_supply(sweep, sums)
+        forward()
         if sweep > 0:
-            send_supply(sweep)
-        forward()
+            send_supply(sweep, True, False)
         for t in range(tiles):
             prune(sweep, t)
-            if sweep == 0 and t == 0:
-                pl.semaphore_wait(barrier, n_dev - 1)
-                send_supply(sweep)
-                for copy in dem_copies:
-                    copy.start()
-            send_payment(sweep, t)
+            if sweep > 0:
+                send_payment(sweep, t)
+        if sweep == 0:
+            pl.semaphore_wait(barrier, n_dev - 1)
+            for t in range(tiles):
+                send_payment(sweep, t)
+            send_supply(sweep, True, False)
+            for copy in dem_copies:
+                copy.start()
+        send_supply(sweep, False, True)
         for t in range(tiles):
             state = jnp.maximum(state, merge(sweep, t))
             reply(t)
@@ -569,7 +577,9 @@
             pltpu.VMEM((tiles, cap_dev + 64, 128), f32),
             pltpu.VMEM((tiles, cap_dev, 128), f32),
             pltpu.VMEM((tiles, cap_dev, 128), f32),
-            pltpu.VMEM((pack, max(cap_dev, n_cap * SLOTS), 128), f32),
+            pltpu.VMEM((tiles, RANGES, cap_dev, 128), f32),
+            pltpu.VMEM((tiles, RANGES + 1, 8, 128), f32),
+            pltpu.VMEM((MERGED_RANGES, n_cap * SLOTS, 128), f32),
             pltpu.VMEM((tiles, cap_dev, 128), f32),
             pltpu.VMEM((5, cap_dev, 128), f32),
             pltpu.VMEM((RANGES + 1, cap_dev, 128), f32),

time: 22 us -> 21.4 us (0.973)
  Pallas kernels: 20.4 us -> 19.9 us
    pallas_call x1, Pallas kernels: 19.4 us -> 18.8 us  [pruned_sweeps(): pl.pallas_call(functools.partial(sweeps_kernel, n_sec, n_cap), out_shape=...]
where the time goes in v3:
time: 21.4 us; the launch traced here: 21.1 us
  Pallas kernels  19.9 us (93%)
  between operations  1.26 us (6%)
    pallas_call x1, Pallas kernels, pruned_sweeps(): pl.pallas_call(functools.partial(sweeps_kernel, n_sec, n_cap), out_shape=...  18.8 us
    pallas_call x1, Pallas kernels, finish(): pl.pallas_call(finish_kernel, grid=(tiles,), out_shape=(jax.ShapeDtypeStr...  1.04 us

profile of v3, /device:TPU:0, one launch (start us, length us, event | category | flops | bytes accessed | tf_op | source)
XLA Modules:
  0.0 21.1 jit_solution(1247191599116731491)
XLA Ops:
  0.6 18.8 %shard_map.90 = (f32[2,576,128]{2,1,0:T(8,128)S(1)}, f32[2,512,128]{2,1,0:T(8,128)S(1)}, f32[2,2,64,128]{3,2,1,0:T(8,128)S(1)}, f32[1,256]{1,0:T(1,128)S(1)}, s32[1]{0:T(128)}) custom-call(f32[8,32,512]{2,1,0:T(8,128)} %start_hbm.1, f32[8,32,512]{2,1,0:T(8,128)} %mass_hbm.1, s32[8,32,512]{2,1,0:T(8,128)} %survive_hbm.1, s32[8]{0:T(128)} %exit_hbm.1, ...), custom_call_target="tpu_custom_call" | custom-call | tf_op jit(solution)/shard_map/pallas_call | solution.py:557
  20.1 1.1 %conditional.1 = (f32[8,32,512]{2,1,0:T(8,128)}, f32[8]{0:T(128)}) conditional(s32[]{:T(128)} %bitcast.64, (f32[2,576,128]{2,1,0:T(8,128)S(1)}, f32[1,256]{1,0:T(1,128)S(1)}) %tuple.75, (s32[8,32,512]{2,1,0:T(8,128)}, s32[8]{0:T(128)}, f32[2,576,128]{2,1,0:T(8,128)S(1)}, f32[1,256]{1,0:T(1,128)S(1)}, ...), branch_computations={%region_0.0_spmd, %region_1.4_spmd, %region_4.9_spmd, %region_8.24... | conditional | flops 191131504 | bytes 93263816 | solution.py:698
  20.1 1.0 %branch_0_fun.1 = (f32[8,32,512]{2,1,0:T(8,128)}, f32[1,8]{1,0:T(1,128)}) custom-call(f32[2,576,128]{2,1,0:T(8,128)S(1)} %get-tuple-element.266.flipped_ref, f32[1,256]{1,0:T(1,128)S(1)} %get-tuple-element.267.row_ref), custom_call_target="tpu_custom_call" | custom-call | tf_op jit(solution)/shard_map/cond/branch_0_fun/pallas_call | solution.py:666

commit v4 on v3

--- a/solution.py
+++ b/solution.py
@@ -365,7 +365,7 @@
 
         zero = jnp.zeros((8, 128), f32)
         runs, counts, gains, squares = lax.fori_loop(
-            0, steps, down, (tuple(after[::-1]), zero, (zero,) * CHUNK_SLOTS, (zero,) * CHUNK_SLOTS), unroll=8)
+            0, steps, down, (tuple(after[::-1]), zero, (zero,) * CHUNK_SLOTS, (zero,) * CHUNK_SLOTS), unroll=16)
         base = counts_before(tot_ref, counts, sub)
         for p in range(CHUNK_SLOTS):
             l1_ref[0, p * 8:(p + 1) * 8, :] = gains[p]
@@ -457,7 +457,7 @@
             best_ref[t, rows, :] = jnp.maximum(moved - 1.41 * capital, g_ref[t, rows, :] - 0.91 * capital)
             return carry
 
-        lax.fori_loop(0, steps, one, 0, unroll=8)
+        lax.fori_loop(0, steps, one, 0, unroll=16)
 
     sums = []
     for t in range(tiles):

time: 21.4 us -> 21.2 us (level)
  no operation moved by 1% of the time
where the time goes in v4:
time: 21.2 us; the launch traced here: 21 us
  Pallas kernels  19.7 us (93%)
  between operations  1.26 us (6%)
    pallas_call x1, Pallas kernels, pruned_sweeps(): pl.pallas_call(functools.partial(sweeps_kernel, n_sec, n_cap), out_shape=...  18.7 us
    pallas_call x1, Pallas kernels, finish(): pl.pallas_call(finish_kernel, grid=(tiles,), out_shape=(jax.ShapeDtypeStr...  1.04 us

profile of v4, /device:TPU:0, one launch (start us, length us, event | category | flops | bytes accessed | tf_op | source)
XLA Modules:
  0.0 21.0 jit_solution(12004392937752513888)
XLA Ops:
  0.6 18.7 %shard_map.90 = (f32[2,576,128]{2,1,0:T(8,128)S(1)}, f32[2,512,128]{2,1,0:T(8,128)S(1)}, f32[2,2,64,128]{3,2,1,0:T(8,128)S(1)}, f32[1,256]{1,0:T(1,128)S(1)}, s32[1]{0:T(128)}) custom-call(f32[8,32,512]{2,1,0:T(8,128)} %start_hbm.1, f32[8,32,512]{2,1,0:T(8,128)} %mass_hbm.1, s32[8,32,512]{2,1,0:T(8,128)} %survive_hbm.1, s32[8]{0:T(128)} %exit_hbm.1, ...), custom_call_target="tpu_custom_call" | custom-call | tf_op jit(solution)/shard_map/pallas_call | solution.py:557
  19.9 1.1 %conditional.1 = (f32[8,32,512]{2,1,0:T(8,128)}, f32[8]{0:T(128)}) conditional(s32[]{:T(128)} %bitcast.64, (f32[2,576,128]{2,1,0:T(8,128)S(1)}, f32[1,256]{1,0:T(1,128)S(1)}) %tuple.75, (s32[8,32,512]{2,1,0:T(8,128)}, s32[8]{0:T(128)}, f32[2,576,128]{2,1,0:T(8,128)S(1)}, f32[1,256]{1,0:T(1,128)S(1)}, ...), branch_computations={%region_0.0_spmd, %region_1.4_spmd, %region_4.9_spmd, %region_8.24... | conditional | flops 191131504 | bytes 93263816 | solution.py:698
  19.9 1.0 %branch_0_fun.1 = (f32[8,32,512]{2,1,0:T(8,128)}, f32[1,8]{1,0:T(1,128)}) custom-call(f32[2,576,128]{2,1,0:T(8,128)S(1)} %get-tuple-element.266.flipped_ref, f32[1,256]{1,0:T(1,128)S(1)} %get-tuple-element.267.row_ref), custom_call_target="tpu_custom_call" | custom-call | tf_op jit(solution)/shard_map/cond/branch_0_fun/pallas_call | solution.py:666
